TPU v7x, 8 devices: a whole 2x2x1 slice. The times are simulated.
8 devices in a mesh: rep: 1 (over z), tp: 2 (over y), ep: 4 (over x, core).
Axes of the slice: x: 2, y: 2, z: 1, core: 2. Of those that a mesh axis runs over, the one named last changes fastest.
Arguments:
- hidden: bfloat16 [512, 2048], P(('rep', 'ep'))
- g_attn: float32 [2048], replicated
- w_q: bfloat16 [2048, 2048], P(None, 'tp')
- w_k: bfloat16 [2048, 512], P(None, 'tp')
- w_v: bfloat16 [2048, 512], P(None, 'tp')
- w_o: bfloat16 [2048, 2048], P('tp')
- k_cache: bfloat16 [512, 256, 4, 128], P(('rep', 'ep'), None, 'tp')
- v_cache: bfloat16 [512, 256, 4, 128], P(('rep', 'ep'), None, 'tp')
- lengths: int32 [512], P(('rep', 'ep'))
- g_ffn: float32 [2048], replicated
- ws_gate: bfloat16 [2048, 2816], P(None, 'tp')
- ws_up: bfloat16 [2048, 2816], P(None, 'tp')
- ws_down: bfloat16 [2816, 2048], P('tp')
- w_gate: bfloat16 [64, 2048, 1408], P(('ep', 'tp'))
- w_up: bfloat16 [64, 2048, 1408], P(('ep', 'tp'))
- w_down: bfloat16 [64, 1408, 2048], P(('ep', 'tp'))
- expert_ids: int32 [512, 6], P(('rep', 'ep'))
- gate_vals: float32 [512, 6], P(('rep', 'ep'))
Outputs:
- output: bfloat16 [512, 2048], P(('rep', 'ep'))
All inputs are finite; a program needn't handle non-finite values.
Results may differ from a plain program's by a relative error of at most 0.0135975.
Values are sent between devices in bfloat16 or wider.
A program may use at most 1 GiB of HBM per device.

v0:
```python
import jax
import jax.numpy as jnp
from jax import lax
from jax.sharding import PartitionSpec as P

EPS = 1e-6
CAPACITY = 2


def rms_norm(values, gain):
    return values * lax.rsqrt(jnp.mean(values * values, axis=-1, keepdims=True) + EPS) * gain


def attention_heads(x_norm, w_q, w_k, w_v, k_cache, v_cache, lengths):
    tokens, ctx_len, kv_heads, head_dim = k_cache.shape
    q_heads = w_q.shape[1] // head_dim
    group_size = q_heads // kv_heads
    score_scale = head_dim ** -0.5
    queries = jnp.dot(x_norm, w_q, preferred_element_type=jnp.float32).astype(jnp.bfloat16).reshape(tokens, kv_heads, group_size, head_dim)
    k_new = jnp.dot(x_norm, w_k, preferred_element_type=jnp.float32).astype(jnp.bfloat16).reshape(tokens, kv_heads, head_dim)
    v_new = jnp.dot(x_norm, w_v, preferred_element_type=jnp.float32).astype(jnp.bfloat16).reshape(tokens, kv_heads, head_dim)
    scores = jnp.einsum('tkgd,tskd->tkgs', queries, k_cache, preferred_element_type=jnp.float32) * score_scale
    valid_pos = jnp.arange(ctx_len)[None, None, None, :] < lengths[:, None, None, None]
    scores = jnp.where(valid_pos, scores, -jnp.inf)
    self_score = jnp.einsum('tkgd,tkd->tkg', queries, k_new, preferred_element_type=jnp.float32) * score_scale
    top_score = jnp.maximum(jnp.max(scores, axis=-1), self_score)
    weights = jnp.exp(scores - top_score[..., None])
    self_weight = jnp.exp(self_score - top_score)
    norm_sum = jnp.sum(weights, axis=-1) + self_weight
    mixed_sum = jnp.einsum('tkgs,tskd->tkgd', weights.astype(jnp.bfloat16), v_cache, preferred_element_type=jnp.float32)
    self_term = self_weight.astype(jnp.bfloat16).astype(jnp.float32)[..., None] * v_new.astype(jnp.float32)[:, :, None, :]
    heads_out = ((mixed_sum + self_term) / norm_sum[..., None]).astype(jnp.bfloat16)
    return heads_out.reshape(tokens, q_heads * head_dim)


def swiglu(in_rows, w_in, w_lin, w_out):
    hidden_act = jax.nn.silu(jnp.dot(in_rows, w_in, preferred_element_type=jnp.float32)) * jnp.dot(in_rows, w_lin, preferred_element_type=jnp.float32)
    return jnp.dot(hidden_act.astype(jnp.bfloat16), w_out, preferred_element_type=jnp.float32)


def expert_block(in_rows, slot_gate, w_gate, w_up, w_down):
    up_gate = jnp.einsum('epsd,edf->epsf', in_rows, w_gate, preferred_element_type=jnp.float32)
    up_lin = jnp.einsum('epsd,edf->epsf', in_rows, w_up, preferred_element_type=jnp.float32)
    expert_act = (jax.nn.silu(up_gate) * up_lin).astype(jnp.bfloat16)
    expert_out = jnp.einsum('epsf,efd->epsd', expert_act, w_down, preferred_element_type=jnp.float32)
    return (expert_out * slot_gate[..., None]).astype(jnp.bfloat16)


def dispatch_plan(expert_ids, gate_vals, ep_size, chip_experts, col_index, local_experts, slot_count):
    tokens = expert_ids.shape[0]
    shard_of = expert_ids // chip_experts
    within = expert_ids % chip_experts
    target = (within % local_experts) * ep_size + shard_of
    in_column = (within // local_experts) == col_index
    onehot = (target[:, :, None] == jnp.arange(local_experts * ep_size)) & in_column[:, :, None]
    picked = jnp.any(onehot, axis=1).T
    gate_mat = jnp.sum(jnp.where(onehot, gate_vals[:, :, None], 0.0), axis=1).T
    picked_int = picked.astype(jnp.int32)
    slot_pos = jnp.cumsum(picked_int, axis=1) - picked_int
    placement = picked[:, None, :] & (slot_pos[:, None, :] == jnp.arange(slot_count)[None, :, None])
    slot_gate = jnp.sum(jnp.where(placement, gate_mat[:, None, :], 0.0), axis=-1)
    return (placement.reshape(local_experts, ep_size, slot_count, tokens).astype(jnp.bfloat16),
            slot_gate.reshape(local_experts, ep_size, slot_count))


def solution(mesh):
    ep_size = mesh.shape['ep']
    tp_size = mesh.shape['tp']
    tok_spec = P(('rep', 'ep'), None)
    cache_spec = P(('rep', 'ep'), None, 'tp', None)
    expert_spec = P(('ep', 'tp'), None, None)

    def layer(hidden, g_attn, w_q, w_k, w_v, w_o, k_cache, v_cache, lengths, g_ffn, ws_gate, ws_up, ws_down, w_gate, w_up, w_down, expert_ids, gate_vals):
        h_f32 = hidden.astype(jnp.float32)
        x_norm = rms_norm(h_f32, g_attn).astype(jnp.bfloat16)
        heads_out = attention_heads(x_norm, w_q, w_k, w_v, k_cache, v_cache, lengths)
        attn_part = jnp.dot(heads_out, w_o, preferred_element_type=jnp.float32).astype(jnp.bfloat16)
        attn_f32 = lax.psum(attn_part, 'tp').astype(jnp.float32)
        y_norm = rms_norm(h_f32 + attn_f32, g_ffn).astype(jnp.bfloat16)
        shared_part = swiglu(y_norm, ws_gate, ws_up, ws_down)
        tokens, top_k = expert_ids.shape
        local_experts = w_gate.shape[0]
        num_experts = local_experts * ep_size * tp_size
        slot_count = min(tokens, (CAPACITY * tokens * top_k + num_experts - 1) // num_experts)
        placement, slot_gate = dispatch_plan(expert_ids, gate_vals, ep_size, local_experts * tp_size, lax.axis_index('tp'), local_experts, slot_count)
        send_rows = jnp.einsum('epst,td->epsd', placement, x_norm, preferred_element_type=jnp.float32).astype(jnp.bfloat16)
        recv_rows = lax.all_to_all(send_rows, 'ep', 1, 1, tiled=True)
        recv_gate = lax.all_to_all(slot_gate, 'ep', 1, 1, tiled=True)
        weighted = expert_block(recv_rows, recv_gate, w_gate, w_up, w_down)
        returned = lax.all_to_all(weighted, 'ep', 1, 1, tiled=True)
        routed_part = jnp.einsum('epst,epsd->td', placement, returned, preferred_element_type=jnp.float32)
        ffn_sum = lax.psum((shared_part + routed_part).astype(jnp.bfloat16), 'tp')
        return (h_f32 + attn_f32 + ffn_sum.astype(jnp.float32)).astype(jnp.bfloat16)

    in_specs = (tok_spec, P(None), P(None, 'tp'), P(None, 'tp'), P(None, 'tp'), P('tp', None), cache_spec, cache_spec, P(('rep', 'ep')), P(None), P(None, 'tp'), P(None, 'tp'), P('tp', None), expert_spec, expert_spec, expert_spec, tok_spec, tok_spec)
    return jax.shard_map(layer, mesh=mesh, in_specs=in_specs, out_specs=tok_spec, check_vma=False)
```

profile of v0, /device:TPU:0, one launch (start us, length us, event | category | flops | bytes accessed | tf_op | source)
XLA Modules:
  0.0 216.1 jit_solution(2273676364587784888)
XLA Ops:
  6.5 0.8 fusion.60
  8.1 0.7 select_reduce_fusion.1
  10.0 4.6 %all-to-all-start.1 = ((f32[4,1,192]{2,1,0:T(1,128)}), f32[4,1,192]{2,1,0:T(1,128)S(1)}, u32[]{:S(2)}, u32[]{:S(2)}) async-start(f32[4,1,192]{2,1,0:T(1,128)} %reshape.88), calls=%async_computation.1 | async-start | bytes 8192 | tf_op jit(solution)/shard_map/all_to_all | solution.py:88
  14.6 1.2 fusion.34
  15.9 3.1 %convolution_convert_fusion.2 = bf16[128,1024]{1,0:T(8,128)(2,1)S(1)} fusion(bf16[2048,1024]{1,0:T(8,128)(2,1)} %param.20, bf16[128,2048]{1,0:T(8,128)(2,1)} %param.18, f32[2048]{0:T(1024)} %param.19, f32[128]{0:T(128)S(1)} %add_rsqrt_fusion.1), kind=kOutput, calls=%fused_computation.29 | convolution fusion | flops 538050560 | bytes 4989440 | tf_op jit(solution)/shard_map/dot_general | solution.py:19
  19.0 1.1 convolution_convert_fusion
  20.4 2.1 copy.45
  22.5 5.0 %all-to-all-start = ((bf16[8,4,24,2048]{3,2,0,1:T(8,128)(2,1)}), bf16[8,4,24,2048]{3,2,0,1:T(8,128)(2,1)}, u32[]{:S(2)}, u32[]{:S(2)}) async-start(bf16[8,4,24,2048]{3,2,0,1:T(8,128)(2,1)} %copy.45), calls=%async_computation | async-start | bytes 6291456 | tf_op jit(solution)/shard_map/all_to_all | solution.py:87
  28.7 10.4 %fusion.73 = (f32[128,2,4]{2,1,0:T(2,128)S(1)}, f32[128,2,4,256]{3,2,1,0:T(4,128)S(1)}) fusion(bf16[128,2,4,128]{3,2,1,0:T(4,128)(2,1)S(1)} %reshape.74, bf16[128,256,2,128]{3,2,1,0:T(2,128)(2,1)} %param.24, pred[128,256]{1,0:T(8,128)(4,1)S(1)} %iota_compare_fusion.2), kind=kOutput, calls=%fused_computation.91 | convolution fusion | flops 67894272 | bytes 18124800 | tf_op jit(solution)/shard_map/tkgd,tskd->tkgs/dot_general | solution.py:22
  39.2 0.9 fusion.43
  41.5 22.7 %all-to-all-done = bf16[8,4,24,2048]{3,2,0,1:T(8,128)(2,1)} async-done(((bf16[8,4,24,2048]{3,2,0,1:T(8,128)(2,1)}), bf16[8,4,24,2048]{3,2,0,1:T(8,128)(2,1)}, u32[]{:S(2)}, u32[]{:S(2)}) %all-to-all-start) | async-done | bytes 3145760 | tf_op jit(solution)/shard_map/all_to_all | solution.py:87
  64.2 20.9 %fusion = f32[8,4,24,1408]{3,2,1,0:T(8,128)} fusion(bf16[8,2048,1408]{2,1,0:T(8,128)(2,1)} %param.32, bf16[8,4,24,2048]{3,2,0,1:T(8,128)(2,1)} %all-to-all-done), kind=kOutput, calls=%fused_computation | convolution fusion | flops 4429185024 | bytes 53608448 | tf_op jit(solution)/shard_map/epsd,edf->epsf/dot_general | solution.py:43
  85.1 20.9 %multiply_convert_fusion.1 = bf16[8,4,24,1408]{3,2,1,0:T(8,128)(2,1)} fusion(f32[8,4,24,1408]{3,2,1,0:T(8,128)} %fusion, bf16[8,2048,1408]{2,1,0:T(8,128)(2,1)} %param.31, bf16[8,4,24,2048]{3,2,0,1:T(8,128)(2,1)} %all-to-all-done), kind=kOutput, calls=%fused_computation.11 | convolution fusion | flops 4435673088 | bytes 55771136 | tf_op jit(solution)/shard_map/epsd,edf->epsf/dot_general | solution.py:42
  106.0 20.5 %multiply_convert_fusion = bf16[8,4,24,2048]{3,2,0,1:T(8,128)(2,1)} fusion(bf16[8,1408,2048]{2,1,0:T(8,128)(2,1)} %param.33, f32[8,4,24]{2,0,1:T(8,128)S(1)} %bitcast.61, bf16[8,4,24,1408]{3,2,1,0:T(8,128)(2,1)} %multiply_convert_fusion.1), kind=kOutput, calls=%fused_computation.10 | convolution fusion | flops 4432330752 | bytes 51448832 | tf_op jit(solution)/shard_map/epsf,efd->epsd/dot_general | solution.py:45
  126.4 4.6 %all-to-all-start.2 = ((bf16[8,4,24,2048]{3,2,0,1:T(8,128)(2,1)}), bf16[8,4,24,2048]{3,2,0,1:T(8,128)(2,1)}, u32[]{:S(2)}, u32[]{:S(2)}) async-start(bf16[8,4,24,2048]{3,2,0,1:T(8,128)(2,1)} %multiply_convert_fusion), calls=%async_computation.2 | async-start | bytes 6291456 | tf_op jit(solution)/shard_map/all_to_all | solution.py:90
  131.1 8.1 %fusion.40 = bf16[128,2,4,128]{3,2,1,0:T(4,128)(2,1)S(1)} fusion(bf16[128,256,2,128]{3,2,1,0:T(2,128)(2,1)} %param.25, f32[128,2,4,256]{3,2,1,0:T(4,128)S(1)} %get-tuple-element.8, f32[128,2,4]{2,1,0:T(2,128)S(1)} %multiply_maximum_fusion, f32[128,2,4]{2,1,0:T(2,128)S(1)} %get-tuple-element.6, f32[128,2,128]{2,1,0:T(2,128)S(1)} %reshape.78, ...), kind=kOutput, calls=%fused_computation.42 | convolution fusion | flops 68157440 | bytes 18231296 | tf_op jit(solution)/shard_map/tkgs,tskd->tkgd/dot_general | solution.py:30
  139.4 3.7 %convolution_convert_fusion.1 = bf16[128,2048]{1,0:T(8,128)(2,1)} fusion(bf16[128,1024]{1,0:T(8,128)(2,1)S(1)} %reshape.76, bf16[1024,2048]{1,0:T(8,128)(2,1)} %param.23), kind=kOutput, calls=%fused_computation.22 | convolution fusion | flops 537133056 | bytes 4980736 | tf_op jit(solution)/shard_map/dot_general | solution.py:77
  143.2 24.8 %all-reduce.3.cloned.1.call-done = bf16[128,2048]{1,0:T(8,128)(2,1)} async-done(((bf16[128,2048]{1,0:T(8,128)(2,1)}), bf16[128,2048]{1,0:T(8,128)(2,1)}) %all-reduce.3.cloned.1.call-update) | async-done | bytes 524304 | tf_op jit(solution)/shard_map/psum | solution.py:78
  168.0 1.3 multiply_reduce_fusion
  169.3 3.9 %fusion.68 = f32[128,1408]{1,0:T(8,128)S(1)} fusion(bf16[2048,1408]{1,0:T(8,128)(2,1)} %param.28, bf16[128,2048]{1,0:T(8,128)(2,1)} %all-reduce.3.cloned.1.call-done, bf16[128,2048]{1,0:T(8,128)(2,1)S(1)} %copy-done.2, f32[2048]{0:T(1024)S(1)} %copy-done.5, f32[128]{0:T(128)S(1)} %add_rsqrt_fusion), kind=kOutput, calls=%fused_computation.90 | convolution fusion | flops 739770368 | bytes 7545344 | tf_op jit(solution)/shard_map/dot_general | solution.py:37
  173.2 3.5 %fusion.18 = f32[128,2048]{1,0:T(8,128)} fusion(bf16[8,4,24,2048]{3,2,0,1:T(8,128)(2,1)} %all-to-all-done.2, s32[8,4,128]{2,1,0:T(4,128)S(1)} %bitcast.54, pred[8,4,128]{2,1,0:T(4,128)(4,1)S(1)} %bitcast.57), kind=kOutput, calls=%fused_computation.18 | convolution fusion | flops 402849792 | bytes 4214784 | tf_op jit(solution)/shard_map/epst,epsd->td/dot_general | solution.py:91
  176.7 7.4 %fusion.21 = bf16[128,2048]{1,0:T(8,128)(2,1)} fusion(f32[128,2048]{1,0:T(8,128)} %fusion.18, bf16[1408,2048]{1,0:T(8,128)(2,1)} %param.30, bf16[2048,1408]{1,0:T(8,128)(2,1)} %param.29, f32[128,1408]{1,0:T(8,128)S(1)} %fusion.68, bf16[128,2048]{1,0:T(8,128)(2,1)S(1)} %copy-done.3, bf16[128,2048]{1,0:T(8,128)(2,1)S(1)} %copy-done.2, ...), kind=kOutput, calls=%fused_computation.20 | convolution fusion | flops 1479573504 | bytes 14885376 | tf_op jit(solution)/shard_map/dot_general | solution.py:38
  184.2 23.0 %all-reduce.5.cloned.1.call-done = bf16[128,2048]{1,0:T(8,128)(2,1)} async-done(((bf16[128,2048]{1,0:T(8,128)(2,1)}), bf16[128,2048]{1,0:T(8,128)(2,1)}) %all-reduce.5.cloned.1.call-update) | async-done | bytes 524304 | tf_op jit(solution)/shard_map/psum | solution.py:92
  207.2 2.1 add_convert_fusion
  (45 shorter events, 5.2 us)
Async XLA Ops:
  6.5 13.5 %copy-start = (bf16[2048,256]{1,0:T(8,128)(2,1)S(1)}, bf16[2048,256]{1,0:T(8,128)(2,1)}, u32[]{:S(2)}) copy-start(bf16[2048,256]{1,0:T(8,128)(2,1)} %param.22) | copy-start | bytes 3145732
  6.5 12.5 %copy-start.2 = (bf16[128,2048]{1,0:T(8,128)(2,1)S(1)}, bf16[128,2048]{1,0:T(8,128)(2,1)}, u32[]{:S(2)}) copy-start(bf16[128,2048]{1,0:T(8,128)(2,1)} %param.18) | copy-start | bytes 1572868
  6.5 12.5 %copy-start.4 = (f32[2048]{0:T(1024)S(1)}, f32[2048]{0:T(1024)}, u32[]{:S(2)}) copy-start(f32[2048]{0:T(1024)} %param.19) | copy-start | bytes 24580
  10.0 12.5 %all-to-all-start.1 = ((f32[4,1,192]{2,1,0:T(1,128)}), f32[4,1,192]{2,1,0:T(1,128)S(1)}, u32[]{:S(2)}, u32[]{:S(2)}) async-start(f32[4,1,192]{2,1,0:T(1,128)} %reshape.88), calls=%async_computation.1 | async-start | bytes 8192 | tf_op jit(solution)/shard_map/all_to_all | solution.py:88
  22.5 5.0 %copy-start.7 = (bf16[2048,256]{1,0:T(8,128)(2,1)S(1)}, bf16[2048,256]{1,0:T(8,128)(2,1)}, u32[]{:S(2)}) copy-start(bf16[2048,256]{1,0:T(8,128)(2,1)} %param.21) | copy-start | bytes 3145732
  22.5 5.6 %copy-start.6 = (s32[128]{0:T(128)S(1)}, s32[128]{0:T(128)}, u32[]{:S(2)}) copy-start(s32[128]{0:T(128)} %param.26) | copy-start | bytes 1540
  22.5 41.6 %all-to-all-start = ((bf16[8,4,24,2048]{3,2,0,1:T(8,128)(2,1)}), bf16[8,4,24,2048]{3,2,0,1:T(8,128)(2,1)}, u32[]{:S(2)}, u32[]{:S(2)}) async-start(bf16[8,4,24,2048]{3,2,0,1:T(8,128)(2,1)} %copy.45), calls=%async_computation | async-start | bytes 6291456 | tf_op jit(solution)/shard_map/all_to_all | solution.py:87
  126.4 46.8 %all-to-all-start.2 = ((bf16[8,4,24,2048]{3,2,0,1:T(8,128)(2,1)}), bf16[8,4,24,2048]{3,2,0,1:T(8,128)(2,1)}, u32[]{:S(2)}, u32[]{:S(2)}) async-start(bf16[8,4,24,2048]{3,2,0,1:T(8,128)(2,1)} %multiply_convert_fusion), calls=%async_computation.2 | async-start | bytes 6291456 | tf_op jit(solution)/shard_map/all_to_all | solution.py:90
  131.1 36.9 %all-reduce.3.cloned.1.call-start = ((), (), s32[]{:S(2)}) async-start(), calls=%async_computation.3 | async-start | bytes 1048576 | tf_op jit(solution)/shard_map/psum | solution.py:78
  139.2 30.1 %copy-start.5 = (f32[2048]{0:T(1024)S(1)}, f32[2048]{0:T(1024)}, u32[]{:S(2)}) copy-start(f32[2048]{0:T(1024)} %param.27) | copy-start | bytes 24580
  143.1 64.1 %all-reduce.5.cloned.1.call-start = ((), (), s32[]{:S(2)}) async-start(), calls=%async_computation.4 | async-start | bytes 1048576 | tf_op jit(solution)/shard_map/psum | solution.py:92
  169.3 7.4 %copy-start.3 = (bf16[128,2048]{1,0:T(8,128)(2,1)S(1)}, bf16[128,2048]{1,0:T(8,128)(2,1)}, u32[]{:S(2)}) copy-start(bf16[128,2048]{1,0:T(8,128)(2,1)} %all-reduce.3.cloned.1.call-done) | copy-start | bytes 1572868
  176.7 32.5 %copy-start.1 = (bf16[2048,256]{1,0:T(8,128)(2,1)S(1)}, bf16[2048,256]{1,0:T(8,128)(2,1)}, u32[]{:S(2)}) copy-start(bf16[2048,256]{1,0:T(8,128)(2,1)} %param.22) | copy-start | bytes 3145732
Sparse Core Ops, SparseCore 0:
  143.2 24.6 all-reduce.2
  184.3 22.8 all-reduce.4
where the time goes:
time: 217 us; the launch traced here: 216 us
  matrix products  105 us (48%)
  waiting for transfers between devices  70.6 us (33%)
  starting transfers between devices  14.3 us (7%)
  between operations  13.6 us (6%)
  other arithmetic  9.23 us (4%)
  local copies, waits for them, and re-layouts  3.83 us (2%)
    psum x1, waiting for transfers between devices, layer(): attn_f32 = lax.psum(attn_part, 'tp').astype(jnp.float32)  24.8 us
    psum x1, waiting for transfers between devices, layer(): ffn_sum = lax.psum((shared_part + routed_part).astype(jnp.bfloat16), 'tp')  23 us
    all_to_all x1, waiting for transfers between devices, layer(): recv_rows = lax.all_to_all(send_rows, 'ep', 1, 1, tiled=True)  22.7 us
    dot_general x1, matrix products, expert_block(): jnp.einsum('epsd,edf->epsf', in_rows, w_up, preferred_element_type=jnp.fl...  20.9 us
    dot_general x1, matrix products, expert_block(): jnp.einsum('epsd,edf->epsf', in_rows, w_gate, preferred_element_type=jnp....  20.9 us
    dot_general x1, matrix products, expert_block(): jnp.einsum('epsf,efd->epsd', expert_act, w_down, preferred_element_type=j...  20.5 us
    dot_general x1, matrix products, attention_heads(): jnp.einsum('tkgd,tskd->tkgs', queries, k_cache, preferred_element_type=jn...  10.4 us
    dot_general x1, matrix products, attention_heads(): jnp.einsum('tkgs,tskd->tkgd', weights.astype(jnp.bfloat16), v_cache, pref...  8.08 us
  transfers between devices with their start and end apart: 5, of which 3 were waited for; matrix products, arithmetic and copies ran while one was open for 18% of the time, Pallas kernels for 0%

commit v1 on v0

v1 whole, which is shorter than its diff:
```python
import functools

import jax
import jax.numpy as jnp
from jax import lax
from jax.experimental import pallas as pl
from jax.experimental.pallas import tpu as pltpu
from jax.sharding import PartitionSpec as P

EPS = 1e-6
TILE = 256
SLOT = 32
MESH_ID = pl.DeviceIdType.MESH


def rms_norm(values, gain):
    return values * lax.rsqrt(jnp.mean(values * values, axis=-1, keepdims=True) + EPS) * gain


def attention_heads(x_norm, w_q, w_k, w_v, k_cache, v_cache, lengths):
    tokens, ctx_len, kv_heads, head_dim = k_cache.shape
    q_heads = w_q.shape[1] // head_dim
    group_size = q_heads // kv_heads
    score_scale = head_dim ** -0.5
    queries = jnp.dot(x_norm, w_q, preferred_element_type=jnp.float32).astype(jnp.bfloat16).reshape(tokens, kv_heads, group_size, head_dim)
    k_new = jnp.dot(x_norm, w_k, preferred_element_type=jnp.float32).astype(jnp.bfloat16).reshape(tokens, kv_heads, head_dim)
    v_new = jnp.dot(x_norm, w_v, preferred_element_type=jnp.float32).astype(jnp.bfloat16).reshape(tokens, kv_heads, head_dim)
    scores = jnp.einsum('tkgd,tskd->tkgs', queries, k_cache, preferred_element_type=jnp.float32) * score_scale
    valid_pos = jnp.arange(ctx_len)[None, None, None, :] < lengths[:, None, None, None]
    scores = jnp.where(valid_pos, scores, -jnp.inf)
    self_score = jnp.einsum('tkgd,tkd->tkg', queries, k_new, preferred_element_type=jnp.float32) * score_scale
    top_score = jnp.maximum(jnp.max(scores, axis=-1), self_score)
    weights = jnp.exp(scores - top_score[..., None])
    self_weight = jnp.exp(self_score - top_score)
    norm_sum = jnp.sum(weights, axis=-1) + self_weight
    mixed_sum = jnp.einsum('tkgs,tskd->tkgd', weights.astype(jnp.bfloat16), v_cache, preferred_element_type=jnp.float32)
    self_term = self_weight.astype(jnp.bfloat16).astype(jnp.float32)[..., None] * v_new.astype(jnp.float32)[:, :, None, :]
    heads_out = ((mixed_sum + self_term) / norm_sum[..., None]).astype(jnp.bfloat16)
    return heads_out.reshape(tokens, q_heads * head_dim)


def gate_table(expert_ids, gate_vals, num_experts):
    onehot = expert_ids[:, :, None] == jnp.arange(num_experts)
    return jnp.sum(jnp.where(onehot, gate_vals[:, :, None], 0.0), axis=1).T


def moe_kernel(x_ref, attn_ref, h_ref, gt_ref, gain_ref, wsg_ref, wsu_ref, wsd_ref, wg_ref, wu_ref, wd_ref, out_ref,
               x_all, x_rows, act, place_t, slot_gate, place, y_rows, ring, down, attn_rx, attn_sum, y_norm, gates,
               send1, recv1, send2, recv2, send3, recv3, keep_own, keep_other,
               ring_sem, down_sem, x_ssem, x_rsem, g_ssem, g_rsem, a_sem, s1_sem, r1_sem, s2_sem, r2_sem, s3_sem, r3_sem):
    tp = lax.axis_index('tp')
    ep = lax.axis_index('ep')
    core = ep % 2
    chip = ep // 2
    mate = chip * 2 + 1 - core
    across = (1 - chip) * 2 + core
    diagonal = (1 - chip) * 2 + 1 - core
    tokens, d_model = x_ref.shape
    n_local, _, hidden_dim = wg_ref.shape
    n_tiles = d_model // TILE

    def expert_copies(j, slot):
        return (pltpu.make_async_copy(wg_ref.at[j], ring.at[slot, 0], ring_sem.at[slot, 0]),
                pltpu.make_async_copy(wu_ref.at[j], ring.at[slot, 1], ring_sem.at[slot, 1]))

    def shared_copies(slot):
        return (pltpu.make_async_copy(wsg_ref, ring.at[slot, 0], ring_sem.at[slot, 0]),
                pltpu.make_async_copy(wsu_ref, ring.at[slot, 1], ring_sem.at[slot, 1]))

    def down_copies(i, slot):
        cols = pl.ds(pl.multiple_of(i * TILE, TILE), TILE)
        return (pltpu.make_async_copy(wd_ref.at[:, :, cols], down.at[slot, pl.ds(0, n_local)], down_sem.at[slot, 0]),
                pltpu.make_async_copy(wsd_ref.at[:, cols], down.at[slot, n_local], down_sem.at[slot, 1]))

    def start(copies):
        for c in copies:
            c.start()

    def wait(copies):
        for c in copies:
            c.wait()

    start(expert_copies(0, 0))
    start(expert_copies(1, 1))

    barrier = pltpu.get_barrier_semaphore()
    for dev in ({'ep': mate}, {'ep': across}, {'ep': diagonal}, {'tp': 1 - tp}):
        pl.semaphore_signal(barrier, inc=1, device_id=dev, device_id_type=MESH_ID)
    pl.semaphore_wait(barrier, 4)

    def remote(src, dst, ssem, rsem, dev):
        return pltpu.make_async_remote_copy(src_ref=src, dst_ref=dst, send_sem=ssem, recv_sem=rsem, device_id=dev, device_id_type=MESH_ID)

    def gate_rows(shard):
        return gt_ref.at[pl.ds(pl.multiple_of((shard * 2 + tp) * n_local, n_local), n_local)]

    g_sends = [remote(gate_rows(peer), gates.at[ep], g_ssem.at[k], g_rsem.at[ep], {'ep': peer}) for k, peer in enumerate((mate, across, diagonal))]
    x_sends = [remote(x_ref, x_all.at[ep], x_ssem.at[k], x_rsem.at[ep], {'ep': peer}) for k, peer in enumerate((mate, across))]
    a_send = remote(attn_ref, attn_rx, a_sem.at[0], a_sem.at[1], {'tp': 1 - tp})
    start(g_sends)
    start(x_sends)
    a_send.start()

    def recv_wait(dst, sem):
        pltpu.make_async_copy(dst, dst, sem).wait()

    lane = lax.broadcasted_iota(jnp.int32, (tokens, tokens), 1)
    row = lax.broadcasted_iota(jnp.int32, (tokens, tokens), 0)
    before = (row < lane).astype(jnp.bfloat16)
    slot_row = lax.broadcasted_iota(jnp.int32, (SLOT, tokens), 0).astype(jnp.float32)

    def dispatch(s, block):
        rows = pl.ds(pl.multiple_of(s * SLOT, SLOT), SLOT)
        gate = gates[s]
        chosen = (gate > 0.0).astype(jnp.float32)
        pos = jnp.dot(chosen.astype(jnp.bfloat16), before, preferred_element_type=jnp.float32)
        for j in range(n_local):
            hit = (pos[j:j + 1, :] == slot_row) & (chosen[j:j + 1, :] > 0.0)
            place[j * SLOT:(j + 1) * SLOT, :] = jnp.where(hit, 1.0, 0.0)
            picked = jnp.sum(jnp.where(hit, gate[j:j + 1, :], 0.0), axis=-1, keepdims=True)
            slot_gate[j, rows, :] = jnp.broadcast_to(picked, (SLOT, tokens))
        placed = place[...]
        place_t[s] = placed.T.astype(jnp.bfloat16)
        placed = placed.astype(jnp.bfloat16)

        def gather(n, carry):
            cols = pl.ds(pl.multiple_of(n * TILE, TILE), TILE)
            got = jnp.dot(placed, block[:, cols], preferred_element_type=jnp.float32).astype(jnp.bfloat16)
            x_rows[:, rows, cols] = got.reshape(n_local, SLOT, TILE)
            return carry
        lax.fori_loop(0, n_tiles, gather, 0)

    gates[ep] = gt_ref[pl.ds(pl.multiple_of((ep * 2 + tp) * n_local, n_local), n_local), :]
    dispatch(ep, x_ref)
    for src in (mate, across, diagonal):
        recv_wait(gates.at[src], g_rsem.at[src])
    recv_wait(x_all.at[mate], x_rsem.at[mate])
    dispatch(mate, x_all.at[mate])
    recv_wait(x_all.at[across], x_rsem.at[across])
    x_fwd = remote(x_all.at[across], x_all.at[across], x_ssem.at[2], x_rsem.at[across], {'ep': mate})
    x_fwd.start()
    dispatch(across, x_all.at[across])
    recv_wait(x_all.at[diagonal], x_rsem.at[diagonal])
    dispatch(diagonal, x_all.at[diagonal])

    def gate_up(lhs, slot, dst):
        def part(cols):
            rows = lhs[...]
            g = jnp.dot(rows, ring[slot, 0, :, cols], preferred_element_type=jnp.float32)
            u = jnp.dot(rows, ring[slot, 1, :, cols], preferred_element_type=jnp.float32)
            act[dst, :, cols] = (jax.nn.silu(g) * u).astype(jnp.bfloat16)

        def step(n, carry):
            part(pl.ds(pl.multiple_of(n * TILE, TILE), TILE))
            return carry
        full = hidden_dim // TILE
        lax.fori_loop(0, full, step, 0)
        if hidden_dim % TILE:
            part(pl.ds(full * TILE, hidden_dim - full * TILE))

    def expert(j, carry):
        slot = j % 2
        wait(expert_copies(j, slot))
        gate_up(x_rows.at[j], slot, j)

        @pl.when(j + 2 < n_local)
        def _():
            start(expert_copies(j + 2, slot))

        @pl.when(j + 2 == n_local)
        def _():
            start(shared_copies(slot))
        return carry
    lax.fori_loop(0, n_local, expert, 0)
    shared_slot = n_local % 2
    start(down_copies(0, 0))

    recv_wait(attn_rx, a_sem.at[1])
    block_rows = 16

    def ffn_norm(r, carry):
        rows = pl.ds(pl.multiple_of(r * block_rows, block_rows), block_rows)
        attn = (attn_ref[rows, :].astype(jnp.float32) + attn_rx[rows, :].astype(jnp.float32)).astype(jnp.bfloat16).astype(jnp.float32)
        res = h_ref[rows, :].astype(jnp.float32) + attn
        attn_sum[rows, :] = res
        y_norm[rows, :] = rms_norm(res, gain_ref[...]).astype(jnp.bfloat16)
        return carry
    lax.fori_loop(0, tokens // block_rows, ffn_norm, 0)
    wait(shared_copies(shared_slot))
    gate_up(y_norm, shared_slot, n_local)
    start(down_copies(1, 1))

    def split3(v):
        a = v.astype(jnp.bfloat16)
        r = v - a.astype(jnp.float32)
        b = r.astype(jnp.bfloat16)
        c = (r - b.astype(jnp.float32)).astype(jnp.bfloat16)
        return a, b, c

    def combine(s):
        rows = pl.ds(pl.multiple_of(s * SLOT, SLOT), SLOT)
        parts = split3(y_rows[:, rows, :].reshape(n_local * SLOT, TILE))
        onehot = place_t[s]
        sums = [jnp.dot(onehot, p, preferred_element_type=jnp.float32) for p in parts]
        return sums[0] + (sums[1] + sums[2])

    def s1_copy(i):
        return remote(send1.at[i], recv1.at[i], s1_sem.at[i], r1_sem.at[i], {'ep': mate})

    def s2_copy(i):
        return remote(send2.at[i], recv2.at[i], s2_sem.at[i], r2_sem.at[i], {'ep': across})

    def s3_copy(i):
        return remote(send3.at[i], recv3.at[i], s3_sem.at[i], r3_sem.at[i], {'tp': 1 - tp})

    def down_tile(i, slot):
        wait(down_copies(i, slot))

        def one(j, carry):
            out = jnp.dot(act[j], down[slot, j], preferred_element_type=jnp.float32)
            gate = slot_gate[j]
            y_rows[j] = out * jnp.concatenate([gate] * (TILE // tokens), axis=-1)
            return carry
        lax.fori_loop(0, n_local, one, 0)
        for b in range(2):
            send1[i, b] = combine(b * 2 + 1 - core).astype(jnp.bfloat16)
        s1_copy(i).start()
        keep_other[i] = combine((1 - chip) * 2 + core)
        keep_own[i] = combine(ep) + jnp.dot(act[n_local], down[slot, n_local], preferred_element_type=jnp.float32)

        @pl.when(i + 2 < n_tiles)
        def _():
            start(down_copies(i + 2, slot))

    def step(i, carry):
        @pl.when(i < n_tiles)
        def _():
            down_tile(i, i % 2)

        @pl.when((i >= LAG1) & (i < n_tiles + LAG1))
        def _():
            k = i - LAG1
            recv_wait(recv1.at[k], r1_sem.at[k])
            send2[k] = (keep_other[k] + recv1[k, 1 - chip].astype(jnp.float32)).astype(jnp.bfloat16)
            s2_copy(k).start()
            keep_own[k] = keep_own[k] + recv1[k, chip].astype(jnp.float32)

        @pl.when((i >= LAG2) & (i < n_tiles + LAG2))
        def _():
            k = i - LAG2
            recv_wait(recv2.at[k], r2_sem.at[k])
            send3[k] = (keep_own[k] + recv2[k].astype(jnp.float32)).astype(jnp.bfloat16)
            s3_copy(k).start()

        @pl.when(i >= LAG3)
        def _():
            k = i - LAG3
            cols = pl.ds(pl.multiple_of(k * TILE, TILE), TILE)
            recv_wait(recv3.at[k], r3_sem.at[k])
            ffn = send3[k].astype(jnp.float32) + recv3[k].astype(jnp.float32)
            out_ref[:, cols] = (attn_sum[:, cols] + ffn).astype(jnp.bfloat16)
        return carry
    lax.fori_loop(0, n_tiles + LAG3, step, 0)

    for c in g_sends + x_sends + [x_fwd, a_send]:
        c.wait_send()

    def drain(i, carry):
        s1_copy(i).wait_send()
        s2_copy(i).wait_send()
        s3_copy(i).wait_send()
        return carry
    lax.fori_loop(0, n_tiles, drain, 0)


LAG1, LAG2, LAG3 = 1, 4, 7


def moe(x_norm, attn_part, hidden, gates, g_ffn, ws_gate, ws_up, ws_down, w_gate, w_up, w_down):
    tokens, d_model = x_norm.shape
    n_local, _, hidden_dim = w_gate.shape
    n_tiles = d_model // TILE
    bf16, f32 = jnp.bfloat16, jnp.float32
    dma = pltpu.SemaphoreType.DMA
    vmem = pl.BlockSpec(memory_space=pltpu.VMEM)
    hbm = pl.BlockSpec(memory_space=pltpu.HBM)
    return pl.pallas_call(
        moe_kernel,
        out_shape=jax.ShapeDtypeStruct((tokens, d_model), bf16),
        in_specs=[vmem] * 5 + [hbm] * 6,
        out_specs=vmem,
        scratch_shapes=[
            pltpu.VMEM((4, tokens, d_model), bf16),
            pltpu.VMEM((n_local, 4 * SLOT, d_model), bf16),
            pltpu.VMEM((n_local + 1, tokens, hidden_dim), bf16),
            pltpu.VMEM((4, tokens, n_local * SLOT), bf16),
            pltpu.VMEM((n_local, 4 * SLOT, tokens), f32),
            pltpu.VMEM((n_local * SLOT, tokens), f32),
            pltpu.VMEM((n_local, 4 * SLOT, TILE), f32),
            pltpu.VMEM((2, 2, d_model, hidden_dim), bf16),
            pltpu.VMEM((2, n_local + 1, hidden_dim, TILE), bf16),
            pltpu.VMEM((tokens, d_model), bf16),
            pltpu.VMEM((tokens, d_model), f32),
            pltpu.VMEM((tokens, d_model), bf16),
            pltpu.VMEM((4, n_local, tokens), f32),
            pltpu.VMEM((n_tiles, 2, tokens, TILE), bf16),
            pltpu.VMEM((n_tiles, 2, tokens, TILE), bf16),
            pltpu.VMEM((n_tiles, tokens, TILE), bf16),
            pltpu.VMEM((n_tiles, tokens, TILE), bf16),
            pltpu.VMEM((n_tiles, tokens, TILE), bf16),
            pltpu.VMEM((n_tiles, tokens, TILE), bf16),
            pltpu.VMEM((n_tiles, tokens, TILE), f32),
            pltpu.VMEM((n_tiles, tokens, TILE), f32),
            dma((2, 2)), dma((2, 2)), dma((3,)), dma((4,)), dma((3,)), dma((4,)), dma((2,)),
        ] + [dma((n_tiles,))] * 6,
        compiler_params=pltpu.CompilerParams(collective_id=0, has_side_effects=True, vmem_limit_bytes=66 * 1024 * 1024 - 2 * 1024 * 1024 - 1024 * 1024),
        cost_estimate=pl.CostEstimate(flops=2 * tokens * (n_local + 1) * 3 * d_model * hidden_dim, bytes_accessed=(n_local + 1) * 6 * d_model * hidden_dim, transcendentals=0),
        name='moe',
    )(x_norm, attn_part, hidden, gates, g_ffn.reshape(1, d_model), ws_gate, ws_up, ws_down, w_gate, w_up, w_down)


def solution(mesh):
    tok_spec = P(('rep', 'ep'), None)
    cache_spec = P(('rep', 'ep'), None, 'tp', None)
    expert_spec = P(('ep', 'tp'), None, None)
    num_shards = mesh.shape['ep'] * mesh.shape['tp']

    def layer(hidden, g_attn, w_q, w_k, w_v, w_o, k_cache, v_cache, lengths, g_ffn, ws_gate, ws_up, ws_down, w_gate, w_up, w_down, expert_ids, gate_vals):
        h_f32 = hidden.astype(jnp.float32)
        x_norm = rms_norm(h_f32, g_attn).astype(jnp.bfloat16)
        heads_out = attention_heads(x_norm, w_q, w_k, w_v, k_cache, v_cache, lengths)
        attn_part = jnp.dot(heads_out, w_o, preferred_element_type=jnp.float32).astype(jnp.bfloat16)
        gates = gate_table(expert_ids, gate_vals, w_gate.shape[0] * num_shards)
        return moe(x_norm, attn_part, hidden, gates, g_ffn, ws_gate, ws_up, ws_down, w_gate, w_up, w_down)

    in_specs = (tok_spec, P(None), P(None, 'tp'), P(None, 'tp'), P(None, 'tp'), P('tp', None), cache_spec, cache_spec, P(('rep', 'ep')), P(None), P(None, 'tp'), P(None, 'tp'), P('tp', None), expert_spec, expert_spec, expert_spec, tok_spec, tok_spec)
    return jax.shard_map(layer, mesh=mesh, in_specs=in_specs, out_specs=tok_spec, check_vma=False)
```

time: 217 us -> 124 us (0.57)
  Pallas kernels: 0 us -> 88.3 us
  matrix products: 105 us -> 27.7 us
  waiting for transfers between devices: 70.6 us -> 0 us
  starting transfers between devices: 14.3 us -> 0 us
  between operations: 13.6 us -> 0.14 us
  other arithmetic: 9.23 us -> 5.04 us
    pallas_call x0 -> x1, Pallas kernels: none -> 88.3 us  [moe(): pl.pallas_call(moe_kernel, out_shape=jax.ShapeDtypeStruct((tokens, d_mode...]
    dot_general x7 -> x0, matrix products: 78.1 us -> none  [the longest x1 20.9 us: expert_block(): jnp.einsum('epsd,edf->epsf', in_rows, w_up, preferred_element_type=jnp.fl...]
    psum x2 -> x0, waiting for transfers between devices: 47.8 us -> none  [the longest x1 24.8 us: layer(): attn_f32 = lax.psum(attn_part, 'tp').astype(jnp.float32)]
    all_to_all x3 -> x0, waiting for transfers between devices: 22.7 us -> none  [the longest x1 22.7 us: layer(): recv_rows = lax.all_to_all(send_rows, 'ep', 1, 1, tiled=True)]
    all_to_all x3 -> x0, starting transfers between devices: 14.2 us -> none  [the longest x1 4.97 us: layer(): recv_rows = lax.all_to_all(send_rows, 'ep', 1, 1, tiled=True)]
  transfers between devices with their start and end apart: 5 -> 0, of which waited for: 3 -> 0; matrix products, arithmetic and copies ran while one was open for 18% -> 0% of each run, Pallas kernels for 0% -> 0%
where the time goes in v1:
time: 124 us; the launch traced here: 123 us
  Pallas kernels  88.3 us (71%)
  matrix products  27.7 us (22%)
  other arithmetic  5.04 us (4%)
  local copies, waits for them, and re-layouts  2.35 us (2%)
    pallas_call x1, Pallas kernels, moe(): pl.pallas_call(moe_kernel, out_shape=jax.ShapeDtypeStruct((tokens, d_mode...  88.3 us
    dot_general x1, matrix products, attention_heads(): jnp.einsum('tkgd,tskd->tkgs', queries, k_cache, preferred_element_type=jn...  10.4 us
    dot_general x1, matrix products, attention_heads(): jnp.einsum('tkgs,tskd->tkgd', weights.astype(jnp.bfloat16), v_cache, pref...  8.26 us
    dot_general x1, matrix products, layer(): jnp.dot(heads_out, w_o, preferred_element_type=jnp.float32)  3.7 us
    dot_general x1, matrix products, attention_heads(): jnp.dot(x_norm, w_q, preferred_element_type=jnp.float32)  3.09 us

profile of v1, /device:TPU:0, one launch (start us, length us, event | category | flops | bytes accessed | tf_op | source)
XLA Modules:
  0.0 123.5 jit_solution(11282736153277805628)
XLA Ops:
  0.0 1.3 %fusion.14 = f32[128]{0:T(128)S(1)} fusion(bf16[128,2048]{1,0:T(8,128)(2,1)} %h_ref.1), kind=kLoop, calls=%fused_computation.14 | loop fusion | flops 786304 | bytes 524800 | tf_op jit(solution)/shard_map/reduce_sum | solution.py:17
  1.3 1.2 %fusion.16.x_ref = bf16[128,2048]{1,0:T(8,128)(2,1)S(1)} fusion(bf16[128,2048]{1,0:T(8,128)(2,1)} %h_ref.1, f32[2048]{0:T(1024)} %param.19, f32[128]{0:T(128)S(1)} %add_rsqrt_fusion), kind=kLoop, calls=%fused_computation.16 | loop fusion | flops 1048576 | bytes 1057280 | tf_op jit(solution)/shard_map/convert_element_type | solution.py:330
  2.6 0.0 copy-start
  2.6 3.1 %convolution_convert_fusion.1 = bf16[128,1024]{1,0:T(8,128)(2,1)S(1)} fusion(bf16[128,2048]{1,0:T(8,128)(2,1)S(1)} %fusion.16.x_ref, bf16[2048,1024]{1,0:T(8,128)(2,1)} %param.20), kind=kOutput, calls=%fused_computation.9 | convolution fusion | flops 537001984 | bytes 4980736 | tf_op jit(solution)/shard_map/dot_general | solution.py:25
  5.7 0.2 reshape.55
  5.9 1.5 %convolution_convert_fusion.3 = bf16[128,256]{1,0:T(8,128)(2,1)S(1)} fusion(bf16[128,2048]{1,0:T(8,128)(2,1)S(1)} %fusion.16.x_ref, bf16[2048,256]{1,0:T(8,128)(2,1)} %param.21), kind=kOutput, calls=%fused_computation.12 | convolution fusion | flops 134250496 | bytes 1638400 | tf_op jit(solution)/shard_map/dot_general | solution.py:26
  7.4 0.4 fusion.29
  7.8 0.7 iota_compare_fusion.1
  8.6 10.4 %fusion.28 = (f32[128,2,4]{2,1,0:T(2,128)S(1)}, f32[128,2,4,256]{3,2,1,0:T(4,128)S(1)}) fusion(bf16[128,2,4,128]{3,2,1,0:T(4,128)(2,1)S(1)} %reshape.55, bf16[128,256,2,128]{3,2,1,0:T(2,128)(2,1)} %param.24, pred[128,256]{1,0:T(8,128)(4,1)S(1)} %iota_compare_fusion.1), kind=kOutput, calls=%fused_computation.31 | convolution fusion | flops 67894272 | bytes 18124800 | tf_op jit(solution)/shard_map/tkgd,tskd->tkgs/dot_general | solution.py:28
  19.0 0.1 multiply_maximum_fusion
  19.1 0.9 fusion.23
  19.9 0.2 convert_convert_fusion
  20.1 0.0 copy-done.1
  20.1 0.3 fusion.10
  20.4 0.1 reshape.59
  20.5 0.0 copy-start.2
  20.5 0.0 copy-start.3
  20.5 8.3 %fusion.20 = bf16[128,2,4,128]{3,2,1,0:T(4,128)(2,1)S(1)} fusion(bf16[128,256,2,128]{3,2,1,0:T(2,128)(2,1)} %param.25, f32[128,2,4,256]{3,2,1,0:T(4,128)S(1)} %get-tuple-element.8, f32[128,2,4]{2,1,0:T(2,128)S(1)} %multiply_maximum_fusion, f32[128,2,4]{2,1,0:T(2,128)S(1)} %get-tuple-element.6, f32[128,2,128]{2,1,0:T(2,128)S(1)} %reshape.59, ...), kind=kOutput, calls=%fused_computation.19 | convolution fusion | flops 68157440 | bytes 18231296 | tf_op jit(solution)/shard_map/tkgs,tskd->tkgd/dot_general | solution.py:36
  28.8 0.0 copy-done
  28.8 0.2 reshape.57
  29.0 3.7 %convolution_convert_fusion.attn_ref = bf16[128,2048]{1,0:T(8,128)(2,1)} fusion(bf16[128,1024]{1,0:T(8,128)(2,1)S(1)} %reshape.57, bf16[1024,2048]{1,0:T(8,128)(2,1)} %param.23), kind=kOutput, calls=%fused_computation.4 | convolution fusion | flops 537133056 | bytes 4980736 | tf_op jit(solution)/shard_map/dot_general | solution.py:332
  32.7 0.6 select_reduce_fusion
  33.3 88.3 %moe.1 = bf16[128,2048]{1,0:T(8,128)(2,1)} custom-call(bf16[128,2048]{1,0:T(8,128)(2,1)} %copy-done, bf16[128,2048]{1,0:T(8,128)(2,1)} %convolution_convert_fusion.attn_ref, bf16[128,2048]{1,0:T(8,128)(2,1)} %h_ref.1, f32[64,128]{1,0:T(8,128)} %bitcast.17, f32[1,2048]{1,0:T(1,128)} %bitcast.18, bf16[2048,1408]{1,0:T(8,128)(2,1)} %wsg_ref.1, ...), custom_call_target="tpu_custom_call" | custom-call | flops 19931332608 | bytes 155713536 | tf_op jit(solution)/shard_map/moe/pallas_call | solution.py:287
  121.6 1.9 %copy.44 = bf16[128,2048]{1,0:T(8,128)(2,1)} copy(bf16[128,2048]{1,0:T(8,128)(2,1)} %moe.1) | data formatting | bytes 1048576
  (5 shorter events, 0.0 us)
Async XLA Ops:
  0.0 20.1 %copy-start.1 = (bf16[2048,256]{1,0:T(8,128)(2,1)S(1)}, bf16[2048,256]{1,0:T(8,128)(2,1)}, u32[]{:S(2)}) copy-start(bf16[2048,256]{1,0:T(8,128)(2,1)} %param.22) | copy-start | bytes 3145732
  2.6 26.2 %copy-start = (bf16[128,2048]{1,0:T(8,128)(2,1)}, bf16[128,2048]{1,0:T(8,128)(2,1)S(1)}, u32[]{:S(2)}) copy-start(bf16[128,2048]{1,0:T(8,128)(2,1)S(1)} %fusion.16.x_ref) | copy-start | bytes 1572868
  20.5 12.2 %copy-start.2 = (f32[128,6]{0,1:T(8,128)S(1)}, f32[128,6]{0,1:T(8,128)}, u32[]{:S(2)}) copy-start(f32[128,6]{0,1:T(8,128)} %param.35) | copy-start | bytes 9220
  20.5 12.2 %copy-start.3 = (s32[128,6]{0,1:T(8,128)S(1)}, s32[128,6]{0,1:T(8,128)}, u32[]{:S(2)}) copy-start(s32[128,6]{0,1:T(8,128)} %param.34) | copy-start | bytes 9220

commit v2 on v1

--- a/solution.py
+++ b/solution.py
@@ -10,6 +10,10 @@
 EPS = 1e-6
 TILE = 256
 SLOT = 32
+HEAD = 128
+KV_SLOTS = 4
+KV_PAIRS = 4
+LAG1, LAG2, LAG3 = 1, 4, 7
 MESH_ID = pl.DeviceIdType.MESH
 
 
@@ -17,37 +21,11 @@
     return values * lax.rsqrt(jnp.mean(values * values, axis=-1, keepdims=True) + EPS) * gain
 
 
-def attention_heads(x_norm, w_q, w_k, w_v, k_cache, v_cache, lengths):
-    tokens, ctx_len, kv_heads, head_dim = k_cache.shape
-    q_heads = w_q.shape[1] // head_dim
-    group_size = q_heads // kv_heads
-    score_scale = head_dim ** -0.5
-    queries = jnp.dot(x_norm, w_q, preferred_element_type=jnp.float32).astype(jnp.bfloat16).reshape(tokens, kv_heads, group_size, head_dim)
-    k_new = jnp.dot(x_norm, w_k, preferred_element_type=jnp.float32).astype(jnp.bfloat16).reshape(tokens, kv_heads, head_dim)
-    v_new = jnp.dot(x_norm, w_v, preferred_element_type=jnp.float32).astype(jnp.bfloat16).reshape(tokens, kv_heads, head_dim)
-    scores = jnp.einsum('tkgd,tskd->tkgs', queries, k_cache, preferred_element_type=jnp.float32) * score_scale
-    valid_pos = jnp.arange(ctx_len)[None, None, None, :] < lengths[:, None, None, None]
-    scores = jnp.where(valid_pos, scores, -jnp.inf)
-    self_score = jnp.einsum('tkgd,tkd->tkg', queries, k_new, preferred_element_type=jnp.float32) * score_scale
-    top_score = jnp.maximum(jnp.max(scores, axis=-1), self_score)
-    weights = jnp.exp(scores - top_score[..., None])
-    self_weight = jnp.exp(self_score - top_score)
-    norm_sum = jnp.sum(weights, axis=-1) + self_weight
-    mixed_sum = jnp.einsum('tkgs,tskd->tkgd', weights.astype(jnp.bfloat16), v_cache, preferred_element_type=jnp.float32)
-    self_term = self_weight.astype(jnp.bfloat16).astype(jnp.float32)[..., None] * v_new.astype(jnp.float32)[:, :, None, :]
-    heads_out = ((mixed_sum + self_term) / norm_sum[..., None]).astype(jnp.bfloat16)
-    return heads_out.reshape(tokens, q_heads * head_dim)
-
-
-def gate_table(expert_ids, gate_vals, num_experts):
-    onehot = expert_ids[:, :, None] == jnp.arange(num_experts)
-    return jnp.sum(jnp.where(onehot, gate_vals[:, :, None], 0.0), axis=1).T
-
-
-def moe_kernel(x_ref, attn_ref, h_ref, gt_ref, gain_ref, wsg_ref, wsu_ref, wsd_ref, wg_ref, wu_ref, wd_ref, out_ref,
-               x_all, x_rows, act, place_t, slot_gate, place, y_rows, ring, down, attn_rx, attn_sum, y_norm, gates,
-               send1, recv1, send2, recv2, send3, recv3, keep_own, keep_other,
-               ring_sem, down_sem, x_ssem, x_rsem, g_ssem, g_rsem, a_sem, s1_sem, r1_sem, s2_sem, r2_sem, s3_sem, r3_sem):
+def layer_kernel(len_ref, h_ref, gain_a_ref, gain_f_ref, ids_ref, gv_ref, wq_ref, wk_ref, wv_ref, wo_ref, kc_ref, vc_ref,
+                 wsg_ref, wsu_ref, wsd_ref, wg_ref, wu_ref, wd_ref, out_ref,
+                 x_all, x_rows, act, place_t, slot_gate, place, y_rows, ring, down, attn_ref, attn_rx, attn_sum, y_norm, gates, gt_ref,
+                 q_buf, k_buf, v_buf, o_buf, o_rows, send1, recv1, send2, recv2, send3, recv3, keep_own, keep_other,
+                 ring_sem, down_sem, kv_sem, w_sem, x_ssem, x_rsem, g_ssem, g_rsem, a_sem, s1_sem, r1_sem, s2_sem, r2_sem, s3_sem, r3_sem):
     tp = lax.axis_index('tp')
     ep = lax.axis_index('ep')
     core = ep % 2
@@ -55,7 +33,12 @@
     mate = chip * 2 + 1 - core
     across = (1 - chip) * 2 + core
     diagonal = (1 - chip) * 2 + 1 - core
-    tokens, d_model = x_ref.shape
+    tokens, d_model = h_ref.shape
+    n_heads = wq_ref.shape[1] // HEAD
+    n_kv = wk_ref.shape[1] // HEAD
+    group = n_heads // n_kv
+    ctx_rows = kc_ref.shape[1] // 2
+    x_ref = x_all.at[ep]
     n_local, _, hidden_dim = wg_ref.shape
     n_tiles = d_model // TILE
 
@@ -69,8 +52,18 @@
 
     def down_copies(i, slot):
         cols = pl.ds(pl.multiple_of(i * TILE, TILE), TILE)
-        return (pltpu.make_async_copy(wd_ref.at[:, :, cols], down.at[slot, pl.ds(0, n_local)], down_sem.at[slot, 0]),
-                pltpu.make_async_copy(wsd_ref.at[:, cols], down.at[slot, n_local], down_sem.at[slot, 1]))
+        base = slot * (n_local + 1)
+        return (pltpu.make_async_copy(wd_ref.at[:, :, cols], down.at[pl.ds(base, n_local)], down_sem.at[slot, 0]),
+                pltpu.make_async_copy(wsd_ref.at[:, cols], down.at[base + n_local], down_sem.at[slot, 1]))
+
+    def cache_copies(g):
+        slot = g % KV_SLOTS
+        copies = []
+        for k in range(KV_PAIRS):
+            dst = down.at[slot * KV_PAIRS + k, pl.ds(0, 2 * ctx_rows)]
+            for n, ref in enumerate((kc_ref, vc_ref)):
+                copies.append(pltpu.make_async_copy(ref.at[g * KV_PAIRS + k], dst.at[:, pl.ds(n * HEAD, HEAD)], kv_sem.at[slot, k, n]))
+        return copies
 
     def start(copies):
         for c in copies:
@@ -80,12 +73,33 @@
         for c in copies:
             c.wait()
 
-    start(expert_copies(0, 0))
-    start(expert_copies(1, 1))
+    qw, kvw, half = n_heads * HEAD, n_kv * HEAD, d_model // 2
+    proj = (pltpu.make_async_copy(wq_ref, ring.at[0, 0, :, pl.ds(0, qw)], w_sem.at[0]),
+            pltpu.make_async_copy(wk_ref, ring.at[0, 1, :, pl.ds(0, kvw)], w_sem.at[1]),
+            pltpu.make_async_copy(wv_ref, ring.at[0, 1, :, pl.ds(kvw, kvw)], w_sem.at[2]))
+    out_proj = [pltpu.make_async_copy(wo_ref.at[:, pl.ds(b * half, half)], ring.at[1, 0, pl.ds(b * qw, qw), pl.ds(0, half)], w_sem.at[3 + b]) for b in range(2)]
+    start(proj)
+    for g in range(KV_SLOTS):
+        start(cache_copies(g))
+    start(out_proj)
 
     barrier = pltpu.get_barrier_semaphore()
     for dev in ({'ep': mate}, {'ep': across}, {'ep': diagonal}, {'tp': 1 - tp}):
         pl.semaphore_signal(barrier, inc=1, device_id=dev, device_id_type=MESH_ID)
+
+    block_rows = 16
+    expert_row = lax.broadcasted_iota(jnp.int32, gt_ref.shape, 0)
+    table = jnp.zeros(gt_ref.shape, jnp.float32)
+    for j in range(ids_ref.shape[0]):
+        table = table + jnp.where(ids_ref[j:j + 1, :] == expert_row, gv_ref[j:j + 1, :], 0.0)
+    gt_ref[...] = table
+
+    def attn_norm(r, carry):
+        rows = pl.ds(pl.multiple_of(r * block_rows, block_rows), block_rows)
+        x_ref[rows, :] = rms_norm(h_ref[rows, :].astype(jnp.float32), gain_a_ref[...]).astype(jnp.bfloat16)
+        return carry
+    lax.fori_loop(0, tokens // block_rows, attn_norm, 0)
+
     pl.semaphore_wait(barrier, 4)
 
     def remote(src, dst, ssem, rsem, dev):
@@ -99,7 +113,6 @@
     a_send = remote(attn_ref, attn_rx, a_sem.at[0], a_sem.at[1], {'tp': 1 - tp})
     start(g_sends)
     start(x_sends)
-    a_send.start()
 
     def recv_wait(dst, sem):
         pltpu.make_async_copy(dst, dst, sem).wait()
@@ -130,15 +143,70 @@
             return carry
         lax.fori_loop(0, n_tiles, gather, 0)
 
+    x_own = x_ref[...]
+    wait(proj)
+    for n in range(qw // TILE):
+        got = jnp.dot(x_own, ring[0, 0, :, n * TILE:(n + 1) * TILE], preferred_element_type=jnp.float32).astype(jnp.bfloat16).astype(jnp.float32)
+        for k in range(TILE // HEAD):
+            q_buf[:, n * (TILE // HEAD) + k, :] = got[:, k * HEAD:(k + 1) * HEAD]
+    for n, buf in enumerate((k_buf, v_buf)):
+        got = jnp.dot(x_own, ring[0, 1, :, n * kvw:(n + 1) * kvw], preferred_element_type=jnp.float32).astype(jnp.bfloat16).astype(jnp.float32)
+        for k in range(n_heads):
+            buf[:, k, :] = got[:, (k // group) * HEAD:(k // group + 1) * HEAD]
+    start(expert_copies(0, 0))
+
+    scale = HEAD ** -0.5
+    cache_lane = lax.broadcasted_iota(jnp.int32, (n_heads, ctx_rows), 1)
+    head_row = lax.broadcasted_iota(jnp.int32, (n_heads, ctx_rows), 0)
+    cache_pos = jnp.where(cache_lane % n_kv == head_row // group, cache_lane // n_kv, ctx_rows)
+
+    def attend(g, carry):
+        wait(cache_copies(g))
+        base = (g % KV_SLOTS) * KV_PAIRS
+        for u in range(2 * KV_PAIRS):
+            t = g * (2 * KV_PAIRS) + u
+            rows = slice((u % 2) * ctx_rows, (u % 2 + 1) * ctx_rows)
+            unit = base + u // 2
+            q = q_buf[t]
+            s = lax.dot_general(q.astype(jnp.bfloat16), down[unit, rows, 0:HEAD], (((1,), (1,)), ((), ())), preferred_element_type=jnp.float32) * scale
+            s = jnp.where(cache_pos < len_ref[t], s, -jnp.inf)
+            own = jnp.sum(q * k_buf[t], axis=-1, keepdims=True) * scale
+            top = jnp.maximum(jnp.max(s, axis=-1, keepdims=True), own)
+            w = jnp.exp(s - top)
+            w_own = jnp.exp(own - top)
+            norm = jnp.sum(w, axis=-1, keepdims=True) + w_own
+            mixed = jnp.dot(w.astype(jnp.bfloat16), down[unit, rows, HEAD:2 * HEAD], preferred_element_type=jnp.float32)
+            o_buf[t] = (mixed + w_own.astype(jnp.bfloat16).astype(jnp.float32) * v_buf[t]) / norm
+
+        @pl.when(g + KV_SLOTS < tokens // (2 * KV_PAIRS))
+        def _():
+            start(cache_copies(g + KV_SLOTS))
+        return carry
+    lax.fori_loop(0, tokens // (2 * KV_PAIRS), attend, 0)
+
+    recv_wait(x_all.at[across], x_rsem.at[across])
+    x_fwd = remote(x_all.at[across], x_all.at[across], x_ssem.at[2], x_rsem.at[across], {'ep': mate})
+    x_fwd.start()
+
+    for k in range(n_heads):
+        o_rows[:, k * HEAD:(k + 1) * HEAD] = o_buf[:, k, :].astype(jnp.bfloat16)
+    wait(out_proj)
+    for b in range(2):
+        def project(n, carry, b=b):
+            cols = pl.ds(pl.multiple_of(n * TILE, TILE), TILE)
+            got = jnp.dot(o_rows[...], ring[1, 0, pl.ds(b * qw, qw), cols], preferred_element_type=jnp.float32)
+            attn_ref[:, pl.ds(pl.multiple_of(b * half + n * TILE, TILE), TILE)] = got.astype(jnp.bfloat16)
+            return carry
+        lax.fori_loop(0, half // TILE, project, 0)
+    start(expert_copies(1, 1))
+
     gates[ep] = gt_ref[pl.ds(pl.multiple_of((ep * 2 + tp) * n_local, n_local), n_local), :]
     dispatch(ep, x_ref)
     for src in (mate, across, diagonal):
         recv_wait(gates.at[src], g_rsem.at[src])
     recv_wait(x_all.at[mate], x_rsem.at[mate])
     dispatch(mate, x_all.at[mate])
-    recv_wait(x_all.at[across], x_rsem.at[across])
-    x_fwd = remote(x_all.at[across], x_all.at[across], x_ssem.at[2], x_rsem.at[across], {'ep': mate})
-    x_fwd.start()
+    a_send.start()
     dispatch(across, x_all.at[across])
     recv_wait(x_all.at[diagonal], x_rsem.at[diagonal])
     dispatch(diagonal, x_all.at[diagonal])
@@ -176,14 +244,13 @@
     start(down_copies(0, 0))
 
     recv_wait(attn_rx, a_sem.at[1])
-    block_rows = 16
 
     def ffn_norm(r, carry):
         rows = pl.ds(pl.multiple_of(r * block_rows, block_rows), block_rows)
         attn = (attn_ref[rows, :].astype(jnp.float32) + attn_rx[rows, :].astype(jnp.float32)).astype(jnp.bfloat16).astype(jnp.float32)
         res = h_ref[rows, :].astype(jnp.float32) + attn
         attn_sum[rows, :] = res
-        y_norm[rows, :] = rms_norm(res, gain_ref[...]).astype(jnp.bfloat16)
+        y_norm[rows, :] = rms_norm(res, gain_f_ref[...]).astype(jnp.bfloat16)
         return carry
     lax.fori_loop(0, tokens // block_rows, ffn_norm, 0)
     wait(shared_copies(shared_slot))
@@ -217,7 +284,7 @@
         wait(down_copies(i, slot))
 
         def one(j, carry):
-            out = jnp.dot(act[j], down[slot, j], preferred_element_type=jnp.float32)
+            out = jnp.dot(act[j], down[slot * (n_local + 1) + j], preferred_element_type=jnp.float32)
             gate = slot_gate[j]
             y_rows[j] = out * jnp.concatenate([gate] * (TILE // tokens), axis=-1)
             return carry
@@ -226,7 +293,7 @@
             send1[i, b] = combine(b * 2 + 1 - core).astype(jnp.bfloat16)
         s1_copy(i).start()
         keep_other[i] = combine((1 - chip) * 2 + core)
-        keep_own[i] = combine(ep) + jnp.dot(act[n_local], down[slot, n_local], preferred_element_type=jnp.float32)
+        keep_own[i] = combine(ep) + jnp.dot(act[n_local], down[slot * (n_local + 1) + n_local], preferred_element_type=jnp.float32)
 
         @pl.when(i + 2 < n_tiles)
         def _():
@@ -273,21 +340,27 @@
     lax.fori_loop(0, n_tiles, drain, 0)
 
 
-LAG1, LAG2, LAG3 = 1, 4, 7
-
-
-def moe(x_norm, attn_part, hidden, gates, g_ffn, ws_gate, ws_up, ws_down, w_gate, w_up, w_down):
-    tokens, d_model = x_norm.shape
+def fused_layer(hidden, g_attn, w_q, w_k, w_v, w_o, k_cache, v_cache, lengths, g_ffn, ws_gate, ws_up, ws_down, w_gate, w_up, w_down, expert_ids, gate_vals, shards):
+    tokens, d_model = hidden.shape
     n_local, _, hidden_dim = w_gate.shape
     n_tiles = d_model // TILE
+    n_heads = w_q.shape[1] // HEAD
+    ctx_len, n_kv = k_cache.shape[1:3]
     bf16, f32 = jnp.bfloat16, jnp.float32
     dma = pltpu.SemaphoreType.DMA
     vmem = pl.BlockSpec(memory_space=pltpu.VMEM)
     hbm = pl.BlockSpec(memory_space=pltpu.HBM)
+    smem = pl.BlockSpec(memory_space=pltpu.SMEM)
+    tile = pltpu.VMEM((n_tiles, tokens, TILE), bf16)
+    tile_f32 = pltpu.VMEM((n_tiles, tokens, TILE), f32)
+    pair_tile = pltpu.VMEM((n_tiles, 2, tokens, TILE), bf16)
+    rows_bf16 = pltpu.VMEM((tokens, d_model), bf16)
+    heads = pltpu.VMEM((tokens, n_heads, HEAD), f32)
+    caches = [c.reshape(tokens // 2, 2 * ctx_len * n_kv, HEAD) for c in (k_cache, v_cache)]
     return pl.pallas_call(
-        moe_kernel,
+        layer_kernel,
         out_shape=jax.ShapeDtypeStruct((tokens, d_model), bf16),
-        in_specs=[vmem] * 5 + [hbm] * 6,
+        in_specs=[smem] + [vmem] * 5 + [hbm] * 12,
         out_specs=vmem,
         scratch_shapes=[
             pltpu.VMEM((4, tokens, d_model), bf16),
@@ -298,40 +371,27 @@
             pltpu.VMEM((n_local * SLOT, tokens), f32),
             pltpu.VMEM((n_local, 4 * SLOT, TILE), f32),
             pltpu.VMEM((2, 2, d_model, hidden_dim), bf16),
-            pltpu.VMEM((2, n_local + 1, hidden_dim, TILE), bf16),
-            pltpu.VMEM((tokens, d_model), bf16),
+            pltpu.VMEM((2 * (n_local + 1), hidden_dim, TILE), bf16),
+            rows_bf16, rows_bf16,
             pltpu.VMEM((tokens, d_model), f32),
-            pltpu.VMEM((tokens, d_model), bf16),
+            rows_bf16,
             pltpu.VMEM((4, n_local, tokens), f32),
-            pltpu.VMEM((n_tiles, 2, tokens, TILE), bf16),
-            pltpu.VMEM((n_tiles, 2, tokens, TILE), bf16),
-            pltpu.VMEM((n_tiles, tokens, TILE), bf16),
-            pltpu.VMEM((n_tiles, tokens, TILE), bf16),
-            pltpu.VMEM((n_tiles, tokens, TILE), bf16),
-            pltpu.VMEM((n_tiles, tokens, TILE), bf16),
-            pltpu.VMEM((n_tiles, tokens, TILE), f32),
-            pltpu.VMEM((n_tiles, tokens, TILE), f32),
-            dma((2, 2)), dma((2, 2)), dma((3,)), dma((4,)), dma((3,)), dma((4,)), dma((2,)),
+            pltpu.VMEM((n_local * shards, tokens), f32),
+            heads, heads, heads, heads,
+            pltpu.VMEM((tokens, n_heads * HEAD), bf16),
+            pair_tile, pair_tile, tile, tile, tile, tile, tile_f32, tile_f32,
+            dma((2, 2)), dma((2, 2)), dma((KV_SLOTS, KV_PAIRS, 2)), dma((5,)), dma((3,)), dma((4,)), dma((3,)), dma((4,)), dma((2,)),
         ] + [dma((n_tiles,))] * 6,
-        compiler_params=pltpu.CompilerParams(collective_id=0, has_side_effects=True, vmem_limit_bytes=66 * 1024 * 1024 - 2 * 1024 * 1024 - 1024 * 1024),
+        compiler_params=pltpu.CompilerParams(collective_id=0, has_side_effects=True, vmem_limit_bytes=63 * 1024 * 1024),
         cost_estimate=pl.CostEstimate(flops=2 * tokens * (n_local + 1) * 3 * d_model * hidden_dim, bytes_accessed=(n_local + 1) * 6 * d_model * hidden_dim, transcendentals=0),
-        name='moe',
-    )(x_norm, attn_part, hidden, gates, g_ffn.reshape(1, d_model), ws_gate, ws_up, ws_down, w_gate, w_up, w_down)
+        name='layer',
+    )(lengths, hidden, g_attn.reshape(1, d_model), g_ffn.reshape(1, d_model), expert_ids.T, gate_vals.T, w_q, w_k, w_v, w_o, *caches, ws_gate, ws_up, ws_down, w_gate, w_up, w_down)
 
 
 def solution(mesh):
     tok_spec = P(('rep', 'ep'), None)
     cache_spec = P(('rep', 'ep'), None, 'tp', None)
     expert_spec = P(('ep', 'tp'), None, None)
-    num_shards = mesh.shape['ep'] * mesh.shape['tp']
-
-    def layer(hidden, g_attn, w_q, w_k, w_v, w_o, k_cache, v_cache, lengths, g_ffn, ws_gate, ws_up, ws_down, w_gate, w_up, w_down, expert_ids, gate_vals):
-        h_f32 = hidden.astype(jnp.float32)
-        x_norm = rms_norm(h_f32, g_attn).astype(jnp.bfloat16)
-        heads_out = attention_heads(x_norm, w_q, w_k, w_v, k_cache, v_cache, lengths)
-        attn_part = jnp.dot(heads_out, w_o, preferred_element_type=jnp.float32).astype(jnp.bfloat16)
-        gates = gate_table(expert_ids, gate_vals, w_gate.shape[0] * num_shards)
-        return moe(x_norm, attn_part, hidden, gates, g_ffn, ws_gate, ws_up, ws_down, w_gate, w_up, w_down)
-
+    layer = functools.partial(fused_layer, shards=mesh.shape['ep'] * mesh.shape['tp'])
     in_specs = (tok_spec, P(None), P(None, 'tp'), P(None, 'tp'), P(None, 'tp'), P('tp', None), cache_spec, cache_spec, P(('rep', 'ep')), P(None), P(None, 'tp'), P(None, 'tp'), P('tp', None), expert_spec, expert_spec, expert_spec, tok_spec, tok_spec)
     return jax.shard_map(layer, mesh=mesh, in_specs=in_specs, out_specs=tok_spec, check_vma=False)

time: 124 us -> 121 us (0.976)
  Pallas kernels: 88.3 us -> 119 us
  matrix products: 27.7 us -> 0 us
  other arithmetic: 5.04 us -> 0 us
    pallas_call x1, Pallas kernels: 88.3 us -> 119 us  [fused_layer(): pl.pallas_call(layer_kernel, out_shape=jax.ShapeDtypeStruct((tokens, d_mo...]
    dot_general x7 -> x0, matrix products: 27.7 us -> none  [the longest x1 10.4 us: attention_heads(): jnp.einsum('tkgd,tskd->tkgs', queries, k_cache, preferred_element_type=jn...]
    reduce_sum x3 -> x0, other arithmetic: 2.79 us -> none  [the longest x1 1.32 us: rms_norm(): jnp.mean(values * values, axis=-1, keepdims=True) + EPS]
    convert_element_type x2 -> x0, other arithmetic: 1.4 us -> none  [the longest x1 1.24 us: layer(): x_norm = rms_norm(h_f32, g_attn).astype(jnp.bfloat16)]
where the time goes in v2:
time: 121 us
  Pallas kernels  119 us (98%)
  local copies, waits for them, and re-layouts  1.88 us (2%)
    pallas_call x1, Pallas kernels, fused_layer(): pl.pallas_call(layer_kernel, out_shape=jax.ShapeDtypeStruct((tokens, d_mo...  119 us

profile of v2, /device:TPU:0, one launch (start us, length us, event | category | flops | bytes accessed | tf_op | source)
XLA Modules:
  0.0 120.9 jit_solution(4568299957906450961)
XLA Ops:
  0.0 119.1 %layer.1 = bf16[128,2048]{1,0:T(8,128)(2,1)} custom-call(s32[128]{0:T(128)} %len_ref.1, bf16[128,2048]{1,0:T(8,128)(2,1)} %h_ref.1, f32[1,2048]{1,0:T(1,128)} %bitcast.8, f32[1,2048]{1,0:T(1,128)} %bitcast.9, s32[6,128]{1,0:T(8,128)} %bitcast.10, f32[6,128]{1,0:T(8,128)} %bitcast.11, bf16[2048,1024]{1,0:T(8,128)(2,1)} %wq_ref.1, bf16[2048,256]{1,0:T(8,128)(2,1)} %wk_ref.1, ...), custom_call_target="tpu_custom_call" | custom-call | flops 19931332608 | bytes 155713536 | tf_op jit(solution)/shard_map/layer/pallas_call | solution.py:360
  119.1 1.9 %copy.20 = bf16[128,2048]{1,0:T(8,128)(2,1)} copy(bf16[128,2048]{1,0:T(8,128)(2,1)} %layer.1) | data formatting | bytes 1048576

commit v3 on v2

--- a/solution.py
+++ b/solution.py
@@ -23,7 +23,7 @@
 
 def layer_kernel(len_ref, h_ref, gain_a_ref, gain_f_ref, ids_ref, gv_ref, wq_ref, wk_ref, wv_ref, wo_ref, kc_ref, vc_ref,
                  wsg_ref, wsu_ref, wsd_ref, wg_ref, wu_ref, wd_ref, out_ref,
-                 x_all, x_rows, act, place_t, slot_gate, place, y_rows, ring, down, attn_ref, attn_rx, attn_sum, y_norm, gates, gt_ref,
+                 x_all, x_rows, act, place_t, slot_gate, place, y_parts, ring, down, attn_ref, attn_rx, attn_sum, y_norm, gates, gt_ref,
                  q_buf, k_buf, v_buf, o_buf, o_rows, send1, recv1, send2, recv2, send3, recv3, keep_own, keep_other,
                  ring_sem, down_sem, kv_sem, w_sem, x_ssem, x_rsem, g_ssem, g_rsem, a_sem, s1_sem, r1_sem, s2_sem, r2_sem, s3_sem, r3_sem):
     tp = lax.axis_index('tp')
@@ -136,12 +136,10 @@
         place_t[s] = placed.T.astype(jnp.bfloat16)
         placed = placed.astype(jnp.bfloat16)
 
-        def gather(n, carry):
-            cols = pl.ds(pl.multiple_of(n * TILE, TILE), TILE)
+        for n in range(n_tiles):
+            cols = slice(n * TILE, (n + 1) * TILE)
             got = jnp.dot(placed, block[:, cols], preferred_element_type=jnp.float32).astype(jnp.bfloat16)
             x_rows[:, rows, cols] = got.reshape(n_local, SLOT, TILE)
-            return carry
-        lax.fori_loop(0, n_tiles, gather, 0)
 
     x_own = x_ref[...]
     wait(proj)
@@ -192,12 +190,9 @@
         o_rows[:, k * HEAD:(k + 1) * HEAD] = o_buf[:, k, :].astype(jnp.bfloat16)
     wait(out_proj)
     for b in range(2):
-        def project(n, carry, b=b):
-            cols = pl.ds(pl.multiple_of(n * TILE, TILE), TILE)
-            got = jnp.dot(o_rows[...], ring[1, 0, pl.ds(b * qw, qw), cols], preferred_element_type=jnp.float32)
-            attn_ref[:, pl.ds(pl.multiple_of(b * half + n * TILE, TILE), TILE)] = got.astype(jnp.bfloat16)
-            return carry
-        lax.fori_loop(0, half // TILE, project, 0)
+        for n in range(half // TILE):
+            got = jnp.dot(o_rows[...], ring[1, 0, b * qw:(b + 1) * qw, n * TILE:(n + 1) * TILE], preferred_element_type=jnp.float32)
+            attn_ref[:, b * half + n * TILE:b * half + (n + 1) * TILE] = got.astype(jnp.bfloat16)
     start(expert_copies(1, 1))
 
     gates[ep] = gt_ref[pl.ds(pl.multiple_of((ep * 2 + tp) * n_local, n_local), n_local), :]
@@ -212,19 +207,18 @@
     dispatch(diagonal, x_all.at[diagonal])
 
     def gate_up(lhs, slot, dst):
-        def part(cols):
-            rows = lhs[...]
-            g = jnp.dot(rows, ring[slot, 0, :, cols], preferred_element_type=jnp.float32)
-            u = jnp.dot(rows, ring[slot, 1, :, cols], preferred_element_type=jnp.float32)
+        full = hidden_dim // TILE * TILE
+        for c in range(0, full, TILE):
+            cols = slice(c, c + TILE)
+            g = jnp.dot(lhs[...], ring[slot, 0, :, cols], preferred_element_type=jnp.float32)
+            u = jnp.dot(lhs[...], ring[slot, 1, :, cols], preferred_element_type=jnp.float32)
             act[dst, :, cols] = (jax.nn.silu(g) * u).astype(jnp.bfloat16)
-
-        def step(n, carry):
-            part(pl.ds(pl.multiple_of(n * TILE, TILE), TILE))
-            return carry
-        full = hidden_dim // TILE
-        lax.fori_loop(0, full, step, 0)
-        if hidden_dim % TILE:
-            part(pl.ds(full * TILE, hidden_dim - full * TILE))
+        if full < hidden_dim:
+            cols = slice(full, hidden_dim)
+            both = jnp.concatenate([ring[slot, 0, :, cols], ring[slot, 1, :, cols]], axis=1)
+            gu = jnp.dot(lhs[...], both, preferred_element_type=jnp.float32)
+            rest = hidden_dim - full
+            act[dst, :, cols] = (jax.nn.silu(gu[:, :rest]) * gu[:, rest:]).astype(jnp.bfloat16)
 
     def expert(j, carry):
         slot = j % 2
@@ -266,9 +260,7 @@
 
     def combine(s):
         rows = pl.ds(pl.multiple_of(s * SLOT, SLOT), SLOT)
-        parts = split3(y_rows[:, rows, :].reshape(n_local * SLOT, TILE))
-        onehot = place_t[s]
-        sums = [jnp.dot(onehot, p, preferred_element_type=jnp.float32) for p in parts]
+        sums = [jnp.dot(place_t[s], y_parts[p, :, rows, :].reshape(n_local * SLOT, TILE), preferred_element_type=jnp.float32) for p in range(3)]
         return sums[0] + (sums[1] + sums[2])
 
     def s1_copy(i):
@@ -283,12 +275,12 @@
     def down_tile(i, slot):
         wait(down_copies(i, slot))
 
-        def one(j, carry):
+        for j in range(n_local):
             out = jnp.dot(act[j], down[slot * (n_local + 1) + j], preferred_element_type=jnp.float32)
             gate = slot_gate[j]
-            y_rows[j] = out * jnp.concatenate([gate] * (TILE // tokens), axis=-1)
-            return carry
-        lax.fori_loop(0, n_local, one, 0)
+            parts = split3(out * jnp.concatenate([gate] * (TILE // tokens), axis=-1))
+            for p in range(3):
+                y_parts[p, j] = parts[p]
         for b in range(2):
             send1[i, b] = combine(b * 2 + 1 - core).astype(jnp.bfloat16)
         s1_copy(i).start()
@@ -369,7 +361,7 @@
             pltpu.VMEM((4, tokens, n_local * SLOT), bf16),
             pltpu.VMEM((n_local, 4 * SLOT, tokens), f32),
             pltpu.VMEM((n_local * SLOT, tokens), f32),
-            pltpu.VMEM((n_local, 4 * SLOT, TILE), f32),
+            pltpu.VMEM((3, n_local, 4 * SLOT, TILE), bf16),
             pltpu.VMEM((2, 2, d_model, hidden_dim), bf16),
             pltpu.VMEM((2 * (n_local + 1), hidden_dim, TILE), bf16),
             rows_bf16, rows_bf16,

time: 121 us -> 104 us (0.86)
  Pallas kernels: 119 us -> 102 us
    pallas_call x1, Pallas kernels: 119 us -> 102 us  [fused_layer(): pl.pallas_call(layer_kernel, out_shape=jax.ShapeDtypeStruct((tokens, d_mo...]
where the time goes in v3:
time: 104 us
  Pallas kernels  102 us (98%)
  local copies, waits for them, and re-layouts  1.88 us (2%)
    pallas_call x1, Pallas kernels, fused_layer(): pl.pallas_call(layer_kernel, out_shape=jax.ShapeDtypeStruct((tokens, d_mo...  102 us

profile of v3, /device:TPU:0, one launch (start us, length us, event | category | flops | bytes accessed | tf_op | source)
XLA Modules:
  0.0 104.2 jit_solution(4140635224253976956)
XLA Ops:
  0.0 102.3 %layer.1 = bf16[128,2048]{1,0:T(8,128)(2,1)} custom-call(s32[128]{0:T(128)} %len_ref.1, bf16[128,2048]{1,0:T(8,128)(2,1)} %h_ref.1, f32[1,2048]{1,0:T(1,128)} %bitcast.8, f32[1,2048]{1,0:T(1,128)} %bitcast.9, s32[6,128]{1,0:T(8,128)} %bitcast.10, f32[6,128]{1,0:T(8,128)} %bitcast.11, bf16[2048,1024]{1,0:T(8,128)(2,1)} %wq_ref.1, bf16[2048,256]{1,0:T(8,128)(2,1)} %wk_ref.1, ...), custom_call_target="tpu_custom_call" | custom-call | flops 19931332608 | bytes 155713536 | tf_op jit(solution)/shard_map/layer/pallas_call | solution.py:352
  102.3 1.9 %copy.20 = bf16[128,2048]{1,0:T(8,128)(2,1)} copy(bf16[128,2048]{1,0:T(8,128)(2,1)} %layer.1) | data formatting | bytes 1048576

commit v4 on v3

--- a/solution.py
+++ b/solution.py
@@ -13,6 +13,7 @@
 HEAD = 128
 KV_SLOTS = 4
 KV_PAIRS = 4
+BATCH = 4 * KV_PAIRS
 LAG1, LAG2, LAG3 = 1, 4, 7
 MESH_ID = pl.DeviceIdType.MESH
 
@@ -21,11 +22,11 @@
     return values * lax.rsqrt(jnp.mean(values * values, axis=-1, keepdims=True) + EPS) * gain
 
 
-def layer_kernel(len_ref, h_ref, gain_a_ref, gain_f_ref, ids_ref, gv_ref, wq_ref, wk_ref, wv_ref, wo_ref, kc_ref, vc_ref,
+def layer_kernel(len_in, h_in, gain_a_in, gain_f_in, ids_in, gv_in, wq_ref, wk_ref, wv_ref, wo_ref, kc_ref, vc_ref,
                  wsg_ref, wsu_ref, wsd_ref, wg_ref, wu_ref, wd_ref, out_ref,
                  x_all, x_rows, act, place_t, slot_gate, place, y_parts, ring, down, attn_ref, attn_rx, attn_sum, y_norm, gates, gt_ref,
-                 q_buf, k_buf, v_buf, o_buf, o_rows, send1, recv1, send2, recv2, send3, recv3, keep_own, keep_other,
-                 ring_sem, down_sem, kv_sem, w_sem, x_ssem, x_rsem, g_ssem, g_rsem, a_sem, s1_sem, r1_sem, s2_sem, r2_sem, s3_sem, r3_sem):
+                 len_ref, h_ref, gain_a_ref, gain_f_ref, ids_ref, gv_ref, out_buf, q_buf, k_buf, v_buf, o_buf, p_buf, o_rows, send1, recv1, send2, recv2, send3, recv3, keep_own, keep_other,
+                 ring_sem, down_sem, kv_sem, w_sem, x_ssem, x_rsem, g_ssem, g_rsem, a_sem, s1_sem, r1_sem, s2_sem, r2_sem, s3_sem, r3_sem, in_sem, out_sem):
     tp = lax.axis_index('tp')
     ep = lax.axis_index('ep')
     core = ep % 2
@@ -73,20 +74,24 @@
         for c in copies:
             c.wait()
 
-    qw, kvw, half = n_heads * HEAD, n_kv * HEAD, d_model // 2
+    qw, kvw = n_heads * HEAD, n_kv * HEAD
     proj = (pltpu.make_async_copy(wq_ref, ring.at[0, 0, :, pl.ds(0, qw)], w_sem.at[0]),
             pltpu.make_async_copy(wk_ref, ring.at[0, 1, :, pl.ds(0, kvw)], w_sem.at[1]),
             pltpu.make_async_copy(wv_ref, ring.at[0, 1, :, pl.ds(kvw, kvw)], w_sem.at[2]))
-    out_proj = [pltpu.make_async_copy(wo_ref.at[:, pl.ds(b * half, half)], ring.at[1, 0, pl.ds(b * qw, qw), pl.ds(0, half)], w_sem.at[3 + b]) for b in range(2)]
+    out_proj = pltpu.make_async_copy(wo_ref, x_rows, w_sem.at[3])
+    small = [pltpu.make_async_copy(src, dst, in_sem.at[k]) for k, (src, dst) in enumerate(
+        ((h_in, h_ref), (gain_a_in, gain_a_ref), (ids_in, ids_ref), (gv_in, gv_ref), (len_in, len_ref), (gain_f_in, gain_f_ref)))]
+    start(small)
     start(proj)
     for g in range(KV_SLOTS):
         start(cache_copies(g))
-    start(out_proj)
+    out_proj.start()
 
     barrier = pltpu.get_barrier_semaphore()
     for dev in ({'ep': mate}, {'ep': across}, {'ep': diagonal}, {'tp': 1 - tp}):
         pl.semaphore_signal(barrier, inc=1, device_id=dev, device_id_type=MESH_ID)
 
+    wait(small)
     block_rows = 16
     expert_row = lax.broadcasted_iota(jnp.int32, gt_ref.shape, 0)
     table = jnp.zeros(gt_ref.shape, jnp.float32)
@@ -151,36 +156,59 @@
         got = jnp.dot(x_own, ring[0, 1, :, n * kvw:(n + 1) * kvw], preferred_element_type=jnp.float32).astype(jnp.bfloat16).astype(jnp.float32)
         for k in range(n_heads):
             buf[:, k, :] = got[:, (k // group) * HEAD:(k // group + 1) * HEAD]
-    start(expert_copies(0, 0))
 
     scale = HEAD ** -0.5
     cache_lane = lax.broadcasted_iota(jnp.int32, (n_heads, ctx_rows), 1)
     head_row = lax.broadcasted_iota(jnp.int32, (n_heads, ctx_rows), 0)
     cache_pos = jnp.where(cache_lane % n_kv == head_row // group, cache_lane // n_kv, ctx_rows)
 
-    def attend(g, carry):
-        wait(cache_copies(g))
-        base = (g % KV_SLOTS) * KV_PAIRS
-        for u in range(2 * KV_PAIRS):
-            t = g * (2 * KV_PAIRS) + u
-            rows = slice((u % 2) * ctx_rows, (u % 2 + 1) * ctx_rows)
-            unit = base + u // 2
-            q = q_buf[t]
-            s = lax.dot_general(q.astype(jnp.bfloat16), down[unit, rows, 0:HEAD], (((1,), (1,)), ((), ())), preferred_element_type=jnp.float32) * scale
+    def attend(i, carry):
+        for g in range(2):
+            wait(cache_copies(2 * i + g))
+        first = i * BATCH
+        base = (2 * i % KV_SLOTS) * KV_PAIRS
+
+        def cache(u, n):
+            return down[base + u // 2, (u % 2) * ctx_rows:(u % 2 + 1) * ctx_rows, n * HEAD:(n + 1) * HEAD]
+
+        q_all = q_buf[pl.ds(pl.multiple_of(first, BATCH), BATCH)].reshape(BATCH * n_heads, HEAD).astype(jnp.bfloat16)
+        stats = []
+        for u in range(BATCH):
+            t = first + u
+            own_rows = slice(u * n_heads, (u + 1) * n_heads)
+            s = lax.dot_general(q_all, cache(u, 0), (((1,), (1,)), ((), ())), preferred_element_type=jnp.float32)[own_rows] * scale
             s = jnp.where(cache_pos < len_ref[t], s, -jnp.inf)
-            own = jnp.sum(q * k_buf[t], axis=-1, keepdims=True) * scale
+            own = jnp.sum(q_buf[t] * k_buf[t], axis=-1, keepdims=True) * scale
             top = jnp.maximum(jnp.max(s, axis=-1, keepdims=True), own)
             w = jnp.exp(s - top)
             w_own = jnp.exp(own - top)
-            norm = jnp.sum(w, axis=-1, keepdims=True) + w_own
-            mixed = jnp.dot(w.astype(jnp.bfloat16), down[unit, rows, HEAD:2 * HEAD], preferred_element_type=jnp.float32)
-            o_buf[t] = (mixed + w_own.astype(jnp.bfloat16).astype(jnp.float32) * v_buf[t]) / norm
-
-        @pl.when(g + KV_SLOTS < tokens // (2 * KV_PAIRS))
-        def _():
-            start(cache_copies(g + KV_SLOTS))
-        return carry
-    lax.fori_loop(0, tokens // (2 * KV_PAIRS), attend, 0)
+            p_buf[own_rows, :] = w
+            stats.append((w_own, jnp.sum(w, axis=-1, keepdims=True) + w_own))
+        p_all = p_buf[...].astype(jnp.bfloat16)
+        for u in range(0, BATCH, 2):
+            pair = jnp.concatenate([cache(u, 1), cache(u + 1, 1)], axis=1)
+            mixed = jnp.dot(p_all, pair, preferred_element_type=jnp.float32)
+            for e in range(2):
+                w_own, norm = stats[u + e]
+                mine = mixed[(u + e) * n_heads:(u + e + 1) * n_heads, e * HEAD:(e + 1) * HEAD]
+                t = first + u + e
+                o_buf[t] = (mine + w_own.astype(jnp.bfloat16).astype(jnp.float32) * v_buf[t]) / norm
+
+        @pl.when(2 * i + KV_SLOTS < n_groups)
+        def _():
+            for g in range(2):
+                start(cache_copies(2 * i + KV_SLOTS + g))
+
+        @pl.when(i == n_groups // 2 - 4)
+        def _():
+            start(expert_copies(0, 0))
+
+        @pl.when(i == n_groups // 2 - 3)
+        def _():
+            start(expert_copies(1, 1))
+        return carry
+    n_groups = tokens // (2 * KV_PAIRS)
+    lax.fori_loop(0, n_groups // 2, attend, 0)
 
     recv_wait(x_all.at[across], x_rsem.at[across])
     x_fwd = remote(x_all.at[across], x_all.at[across], x_ssem.at[2], x_rsem.at[across], {'ep': mate})
@@ -188,12 +216,11 @@
 
     for k in range(n_heads):
         o_rows[:, k * HEAD:(k + 1) * HEAD] = o_buf[:, k, :].astype(jnp.bfloat16)
-    wait(out_proj)
-    for b in range(2):
-        for n in range(half // TILE):
-            got = jnp.dot(o_rows[...], ring[1, 0, b * qw:(b + 1) * qw, n * TILE:(n + 1) * TILE], preferred_element_type=jnp.float32)
-            attn_ref[:, b * half + n * TILE:b * half + (n + 1) * TILE] = got.astype(jnp.bfloat16)
-    start(expert_copies(1, 1))
+    out_proj.wait()
+    for n in range(n_tiles):
+        cols = slice(n * TILE, (n + 1) * TILE)
+        got = jnp.dot(o_rows[...], x_rows[:, :, cols].reshape(qw, TILE), preferred_element_type=jnp.float32)
+        attn_ref[:, cols] = got.astype(jnp.bfloat16)
 
     gates[ep] = gt_ref[pl.ds(pl.multiple_of((ep * 2 + tp) * n_local, n_local), n_local), :]
     dispatch(ep, x_ref)
@@ -272,6 +299,10 @@
     def s3_copy(i):
         return remote(send3.at[i], recv3.at[i], s3_sem.at[i], r3_sem.at[i], {'tp': 1 - tp})
 
+    def out_copy(i):
+        cols = pl.ds(pl.multiple_of(i * TILE, TILE), TILE)
+        return pltpu.make_async_copy(out_buf.at[:, cols], out_ref.at[:, cols], out_sem.at[i])
+
     def down_tile(i, slot):
         wait(down_copies(i, slot))
 
@@ -317,7 +348,8 @@
             cols = pl.ds(pl.multiple_of(k * TILE, TILE), TILE)
             recv_wait(recv3.at[k], r3_sem.at[k])
             ffn = send3[k].astype(jnp.float32) + recv3[k].astype(jnp.float32)
-            out_ref[:, cols] = (attn_sum[:, cols] + ffn).astype(jnp.bfloat16)
+            out_buf[:, cols] = (attn_sum[:, cols] + ffn).astype(jnp.bfloat16)
+            out_copy(k).start()
         return carry
     lax.fori_loop(0, n_tiles + LAG3, step, 0)
 
@@ -328,6 +360,7 @@
         s1_copy(i).wait_send()
         s2_copy(i).wait_send()
         s3_copy(i).wait_send()
+        out_copy(i).wait()
         return carry
     lax.fori_loop(0, n_tiles, drain, 0)
 
@@ -340,9 +373,7 @@
     ctx_len, n_kv = k_cache.shape[1:3]
     bf16, f32 = jnp.bfloat16, jnp.float32
     dma = pltpu.SemaphoreType.DMA
-    vmem = pl.BlockSpec(memory_space=pltpu.VMEM)
     hbm = pl.BlockSpec(memory_space=pltpu.HBM)
-    smem = pl.BlockSpec(memory_space=pltpu.SMEM)
     tile = pltpu.VMEM((n_tiles, tokens, TILE), bf16)
     tile_f32 = pltpu.VMEM((n_tiles, tokens, TILE), f32)
     pair_tile = pltpu.VMEM((n_tiles, 2, tokens, TILE), bf16)
@@ -352,8 +383,8 @@
     return pl.pallas_call(
         layer_kernel,
         out_shape=jax.ShapeDtypeStruct((tokens, d_model), bf16),
-        in_specs=[smem] + [vmem] * 5 + [hbm] * 12,
-        out_specs=vmem,
+        in_specs=[hbm] * 18,
+        out_specs=hbm,
         scratch_shapes=[
             pltpu.VMEM((4, tokens, d_model), bf16),
             pltpu.VMEM((n_local, 4 * SLOT, d_model), bf16),
@@ -369,15 +400,18 @@
             rows_bf16,
             pltpu.VMEM((4, n_local, tokens), f32),
             pltpu.VMEM((n_local * shards, tokens), f32),
+            pltpu.SMEM((tokens,), jnp.int32), rows_bf16, pltpu.VMEM((1, d_model), f32), pltpu.VMEM((1, d_model), f32),
+            pltpu.VMEM(expert_ids.shape[::-1], jnp.int32), pltpu.VMEM(gate_vals.shape[::-1], f32), rows_bf16,
             heads, heads, heads, heads,
+            pltpu.VMEM((BATCH * n_heads, ctx_len * n_kv), f32),
             pltpu.VMEM((tokens, n_heads * HEAD), bf16),
             pair_tile, pair_tile, tile, tile, tile, tile, tile_f32, tile_f32,
-            dma((2, 2)), dma((2, 2)), dma((KV_SLOTS, KV_PAIRS, 2)), dma((5,)), dma((3,)), dma((4,)), dma((3,)), dma((4,)), dma((2,)),
-        ] + [dma((n_tiles,))] * 6,
+            dma((2, 2)), dma((2, 2)), dma((KV_SLOTS, KV_PAIRS, 2)), dma((4,)), dma((3,)), dma((4,)), dma((3,)), dma((4,)), dma((2,)),
+        ] + [dma((n_tiles,))] * 6 + [dma((6,)), dma((n_tiles,))],
         compiler_params=pltpu.CompilerParams(collective_id=0, has_side_effects=True, vmem_limit_bytes=63 * 1024 * 1024),
         cost_estimate=pl.CostEstimate(flops=2 * tokens * (n_local + 1) * 3 * d_model * hidden_dim, bytes_accessed=(n_local + 1) * 6 * d_model * hidden_dim, transcendentals=0),
         name='layer',
-    )(lengths, hidden, g_attn.reshape(1, d_model), g_ffn.reshape(1, d_model), expert_ids.T, gate_vals.T, w_q, w_k, w_v, w_o, *caches, ws_gate, ws_up, ws_down, w_gate, w_up, w_down)
+    )(lengths, hidden, g_attn.reshape(1, d_model), g_ffn.reshape(1, d_model), expert_ids.T, gate_vals.T, w_q, w_k, w_v, w_o.reshape(n_heads, HEAD, d_model), *caches, ws_gate, ws_up, ws_down, w_gate, w_up, w_down)
 
 
 def solution(mesh):

time: 104 us -> 88.4 us (0.85)
  Pallas kernels: 102 us -> 86.4 us
    pallas_call x1, Pallas kernels: 102 us -> 86.4 us  [fused_layer(): pl.pallas_call(layer_kernel, out_shape=jax.ShapeDtypeStruct((tokens, d_mo...]
where the time goes in v4:
time: 88.4 us; the launch traced here: 88.3 us
  Pallas kernels  86.4 us (98%)
  local copies, waits for them, and re-layouts  1.88 us (2%)
    pallas_call x1, Pallas kernels, fused_layer(): pl.pallas_call(layer_kernel, out_shape=jax.ShapeDtypeStruct((tokens, d_mo...  86.4 us
    unnamed x1, local copies, waits for them, and re-layouts  1.88 us

profile of v4, /device:TPU:0, one launch (start us, length us, event | category | flops | bytes accessed | tf_op | source)
XLA Modules:
  0.0 88.3 jit_solution(1793778832732259246)
XLA Ops:
  0.0 86.4 %layer.1 = bf16[128,2048]{1,0:T(8,128)(2,1)} custom-call(s32[128]{0:T(128)} %len_in.1, bf16[128,2048]{1,0:T(8,128)(2,1)} %h_in.1, f32[1,2048]{1,0:T(1,128)} %bitcast.10, f32[1,2048]{1,0:T(1,128)} %bitcast.11, s32[6,128]{1,0:T(8,128)} %bitcast.12, f32[6,128]{1,0:T(8,128)} %bitcast.13, bf16[2048,1024]{1,0:T(8,128)(2,1)} %wq_ref.1, bf16[2048,256]{1,0:T(8,128)(2,1)} %wk_ref.1, ...), custom_call_target="tpu_custom_call" | custom-call | flops 19931332608 | bytes 155713536 | tf_op jit(solution)/shard_map/layer/pallas_call | solution.py:383
  86.4 1.9 %copy.20 = bf16[128,2048]{1,0:T(8,128)(2,1)} copy(bf16[128,2048]{1,0:T(8,128)(2,1)} %layer.1) | data formatting | bytes 1048576

commit v5 on v4

--- a/solution.py
+++ b/solution.py
@@ -11,9 +11,8 @@
 TILE = 256
 SLOT = 32
 HEAD = 128
-KV_SLOTS = 4
-KV_PAIRS = 4
-BATCH = 4 * KV_PAIRS
+BATCH = 16
+GROUP = 3
 LAG1, LAG2, LAG3 = 1, 4, 7
 MESH_ID = pl.DeviceIdType.MESH
 
@@ -54,16 +53,22 @@
     def down_copies(i, slot):
         cols = pl.ds(pl.multiple_of(i * TILE, TILE), TILE)
         base = slot * (n_local + 1)
-        return (pltpu.make_async_copy(wd_ref.at[:, :, cols], down.at[pl.ds(base, n_local)], down_sem.at[slot, 0]),
-                pltpu.make_async_copy(wsd_ref.at[:, cols], down.at[base + n_local], down_sem.at[slot, 1]))
-
-    def cache_copies(g):
-        slot = g % KV_SLOTS
+        parts = [(j, min(GROUP, n_local - j)) for j in range(0, n_local, GROUP)]
+        copies = [[pltpu.make_async_copy(wd_ref.at[pl.ds(j, n), :, cols], down.at[pl.ds(base + j, n)], down_sem.at[slot, k])] for k, (j, n) in enumerate(parts)]
+        copies[-1].append(pltpu.make_async_copy(wsd_ref.at[:, cols], down.at[base + n_local], down_sem.at[slot, len(parts)]))
+        return copies
+
+    def down_start(i, slot):
+        for part in down_copies(i, slot):
+            start(part)
+
+    def cache_copies(i, n):
+        slot = i % 2
+        pairs = BATCH // 2
         copies = []
-        for k in range(KV_PAIRS):
-            dst = down.at[slot * KV_PAIRS + k, pl.ds(0, 2 * ctx_rows)]
-            for n, ref in enumerate((kc_ref, vc_ref)):
-                copies.append(pltpu.make_async_copy(ref.at[g * KV_PAIRS + k], dst.at[:, pl.ds(n * HEAD, HEAD)], kv_sem.at[slot, k, n]))
+        for k in range(pairs):
+            dst = down.at[slot * pairs + k, pl.ds(0, 2 * ctx_rows)]
+            copies.append(pltpu.make_async_copy((kc_ref, vc_ref)[n].at[i * pairs + k], dst.at[:, pl.ds(n * HEAD, HEAD)], kv_sem.at[slot, k, n]))
         return copies
 
     def start(copies):
@@ -83,8 +88,9 @@
         ((h_in, h_ref), (gain_a_in, gain_a_ref), (ids_in, ids_ref), (gv_in, gv_ref), (len_in, len_ref), (gain_f_in, gain_f_ref)))]
     start(small)
     start(proj)
-    for g in range(KV_SLOTS):
-        start(cache_copies(g))
+    for i in range(2):
+        start(cache_copies(i, 0))
+        start(cache_copies(i, 1))
     out_proj.start()
 
     barrier = pltpu.get_barrier_semaphore()
@@ -163,10 +169,9 @@
     cache_pos = jnp.where(cache_lane % n_kv == head_row // group, cache_lane // n_kv, ctx_rows)
 
     def attend(i, carry):
-        for g in range(2):
-            wait(cache_copies(2 * i + g))
         first = i * BATCH
-        base = (2 * i % KV_SLOTS) * KV_PAIRS
+        base = (i % 2) * (BATCH // 2)
+        wait(cache_copies(i, 0))
 
         def cache(u, n):
             return down[base + u // 2, (u % 2) * ctx_rows:(u % 2 + 1) * ctx_rows, n * HEAD:(n + 1) * HEAD]
@@ -184,6 +189,12 @@
             w_own = jnp.exp(own - top)
             p_buf[own_rows, :] = w
             stats.append((w_own, jnp.sum(w, axis=-1, keepdims=True) + w_own))
+
+        @pl.when(i + 2 < n_batches)
+        def _():
+            start(cache_copies(i + 2, 0))
+
+        wait(cache_copies(i, 1))
         p_all = p_buf[...].astype(jnp.bfloat16)
         for u in range(0, BATCH, 2):
             pair = jnp.concatenate([cache(u, 1), cache(u + 1, 1)], axis=1)
@@ -194,25 +205,17 @@
                 t = first + u + e
                 o_buf[t] = (mine + w_own.astype(jnp.bfloat16).astype(jnp.float32) * v_buf[t]) / norm
 
-        @pl.when(2 * i + KV_SLOTS < n_groups)
-        def _():
-            for g in range(2):
-                start(cache_copies(2 * i + KV_SLOTS + g))
-
-        @pl.when(i == n_groups // 2 - 4)
+        @pl.when(i + 2 < n_batches)
+        def _():
+            start(cache_copies(i + 2, 1))
+
+        @pl.when(i == n_batches - 3)
         def _():
             start(expert_copies(0, 0))
-
-        @pl.when(i == n_groups // 2 - 3)
-        def _():
             start(expert_copies(1, 1))
         return carry
-    n_groups = tokens // (2 * KV_PAIRS)
-    lax.fori_loop(0, n_groups // 2, attend, 0)
-
-    recv_wait(x_all.at[across], x_rsem.at[across])
-    x_fwd = remote(x_all.at[across], x_all.at[across], x_ssem.at[2], x_rsem.at[across], {'ep': mate})
-    x_fwd.start()
+    n_batches = tokens // BATCH
+    lax.fori_loop(0, n_batches, attend, 0)
 
     for k in range(n_heads):
         o_rows[:, k * HEAD:(k + 1) * HEAD] = o_buf[:, k, :].astype(jnp.bfloat16)
@@ -221,6 +224,10 @@
         cols = slice(n * TILE, (n + 1) * TILE)
         got = jnp.dot(o_rows[...], x_rows[:, :, cols].reshape(qw, TILE), preferred_element_type=jnp.float32)
         attn_ref[:, cols] = got.astype(jnp.bfloat16)
+
+    recv_wait(x_all.at[across], x_rsem.at[across])
+    x_fwd = remote(x_all.at[across], x_all.at[across], x_ssem.at[2], x_rsem.at[across], {'ep': mate})
+    x_fwd.start()
 
     gates[ep] = gt_ref[pl.ds(pl.multiple_of((ep * 2 + tp) * n_local, n_local), n_local), :]
     dispatch(ep, x_ref)
@@ -262,7 +269,7 @@
         return carry
     lax.fori_loop(0, n_local, expert, 0)
     shared_slot = n_local % 2
-    start(down_copies(0, 0))
+    down_start(0, 0)
 
     recv_wait(attn_rx, a_sem.at[1])
 
@@ -276,7 +283,7 @@
     lax.fori_loop(0, tokens // block_rows, ffn_norm, 0)
     wait(shared_copies(shared_slot))
     gate_up(y_norm, shared_slot, n_local)
-    start(down_copies(1, 1))
+    down_start(1, 1)
 
     def split3(v):
         a = v.astype(jnp.bfloat16)
@@ -304,23 +311,26 @@
         return pltpu.make_async_copy(out_buf.at[:, cols], out_ref.at[:, cols], out_sem.at[i])
 
     def down_tile(i, slot):
-        wait(down_copies(i, slot))
-
-        for j in range(n_local):
-            out = jnp.dot(act[j], down[slot * (n_local + 1) + j], preferred_element_type=jnp.float32)
-            gate = slot_gate[j]
-            parts = split3(out * jnp.concatenate([gate] * (TILE // tokens), axis=-1))
-            for p in range(3):
-                y_parts[p, j] = parts[p]
+        base = slot * (n_local + 1)
+        now, later = down_copies(i, slot), down_copies(i + 2, slot)
+        for k in range(len(now)):
+            wait(now[k])
+            for j in range(k * GROUP, min((k + 1) * GROUP, n_local)):
+                out = jnp.dot(act[j], down[base + j], preferred_element_type=jnp.float32)
+                parts = split3(out * jnp.concatenate([slot_gate[j]] * (TILE // tokens), axis=-1))
+                for p in range(3):
+                    y_parts[p, j] = parts[p]
+            if k == len(now) - 1:
+                keep_own[i] = jnp.dot(act[n_local], down[base + n_local], preferred_element_type=jnp.float32)
+
+            @pl.when(i + 2 < n_tiles)
+            def _(k=k):
+                start(later[k])
         for b in range(2):
             send1[i, b] = combine(b * 2 + 1 - core).astype(jnp.bfloat16)
         s1_copy(i).start()
         keep_other[i] = combine((1 - chip) * 2 + core)
-        keep_own[i] = combine(ep) + jnp.dot(act[n_local], down[slot * (n_local + 1) + n_local], preferred_element_type=jnp.float32)
-
-        @pl.when(i + 2 < n_tiles)
-        def _():
-            start(down_copies(i + 2, slot))
+        keep_own[i] = keep_own[i] + combine(ep)
 
     def step(i, carry):
         @pl.when(i < n_tiles)
@@ -406,7 +416,7 @@
             pltpu.VMEM((BATCH * n_heads, ctx_len * n_kv), f32),
             pltpu.VMEM((tokens, n_heads * HEAD), bf16),
             pair_tile, pair_tile, tile, tile, tile, tile, tile_f32, tile_f32,
-            dma((2, 2)), dma((2, 2)), dma((KV_SLOTS, KV_PAIRS, 2)), dma((4,)), dma((3,)), dma((4,)), dma((3,)), dma((4,)), dma((2,)),
+            dma((2, 2)), dma((2, 4)), dma((2, BATCH // 2, 2)), dma((4,)), dma((3,)), dma((4,)), dma((3,)), dma((4,)), dma((2,)),
         ] + [dma((n_tiles,))] * 6 + [dma((6,)), dma((n_tiles,))],
         compiler_params=pltpu.CompilerParams(collective_id=0, has_side_effects=True, vmem_limit_bytes=63 * 1024 * 1024),
         cost_estimate=pl.CostEstimate(flops=2 * tokens * (n_local + 1) * 3 * d_model * hidden_dim, bytes_accessed=(n_local + 1) * 6 * d_model * hidden_dim, transcendentals=0),

time: 88.4 us -> 87.4 us (0.989)
  Pallas kernels: 86.4 us -> 85.4 us
    pallas_call x1, Pallas kernels: 86.4 us -> 85.4 us  [fused_layer(): pl.pallas_call(layer_kernel, out_shape=jax.ShapeDtypeStruct((tokens, d_mo...]
where the time goes in v5:
time: 87.4 us; the launch traced here: 87.3 us
  Pallas kernels  85.4 us (98%)
  local copies, waits for them, and re-layouts  1.88 us (2%)
    pallas_call x1, Pallas kernels, fused_layer(): pl.pallas_call(layer_kernel, out_shape=jax.ShapeDtypeStruct((tokens, d_mo...  85.4 us
    unnamed x1, local copies, waits for them, and re-layouts  1.88 us

profile of v5, /device:TPU:0, one launch (start us, length us, event | category | flops | bytes accessed | tf_op | source)
XLA Modules:
  0.0 87.3 jit_solution(4823861624302765918)
XLA Ops:
  0.0 85.4 %layer.1 = bf16[128,2048]{1,0:T(8,128)(2,1)} custom-call(s32[128]{0:T(128)} %len_in.1, bf16[128,2048]{1,0:T(8,128)(2,1)} %h_in.1, f32[1,2048]{1,0:T(1,128)} %bitcast.10, f32[1,2048]{1,0:T(1,128)} %bitcast.11, s32[6,128]{1,0:T(8,128)} %bitcast.12, f32[6,128]{1,0:T(8,128)} %bitcast.13, bf16[2048,1024]{1,0:T(8,128)(2,1)} %wq_ref.1, bf16[2048,256]{1,0:T(8,128)(2,1)} %wk_ref.1, ...), custom_call_target="tpu_custom_call" | custom-call | flops 19931332608 | bytes 155713536 | tf_op jit(solution)/shard_map/layer/pallas_call | solution.py:393
  85.4 1.9 %copy.20 = bf16[128,2048]{1,0:T(8,128)(2,1)} copy(bf16[128,2048]{1,0:T(8,128)(2,1)} %layer.1) | data formatting | bytes 1048576

commit v6 on v5

--- a/solution.py
+++ b/solution.py
@@ -13,6 +13,7 @@
 HEAD = 128
 BATCH = 16
 GROUP = 3
+CHUNKS = 4
 LAG1, LAG2, LAG3 = 1, 4, 7
 MESH_ID = pl.DeviceIdType.MESH
 
@@ -24,8 +25,8 @@
 def layer_kernel(len_in, h_in, gain_a_in, gain_f_in, ids_in, gv_in, wq_ref, wk_ref, wv_ref, wo_ref, kc_ref, vc_ref,
                  wsg_ref, wsu_ref, wsd_ref, wg_ref, wu_ref, wd_ref, out_ref,
                  x_all, x_rows, act, place_t, slot_gate, place, y_parts, ring, down, attn_ref, attn_rx, attn_sum, y_norm, gates, gt_ref,
-                 len_ref, h_ref, gain_a_ref, gain_f_ref, ids_ref, gv_ref, out_buf, q_buf, k_buf, v_buf, o_buf, p_buf, o_rows, send1, recv1, send2, recv2, send3, recv3, keep_own, keep_other,
-                 ring_sem, down_sem, kv_sem, w_sem, x_ssem, x_rsem, g_ssem, g_rsem, a_sem, s1_sem, r1_sem, s2_sem, r2_sem, s3_sem, r3_sem, in_sem, out_sem):
+                 len_ref, h_ref, gain_a_ref, gain_f_ref, ids_ref, gv_ref, q_buf, k_buf, v_buf, o_buf, p_buf, o_rows, send1, recv1, send2, recv2, send3, recv3, keep_own, keep_other,
+                 ring_sem, down_sem, kv_sem, w_sem, x_ssem, x_rsem, g_ssem, g_rsem, a_sem, s1_sem, r1_sem, s2_sem, r2_sem, s3_sem, r3_sem, in_sem):
     tp = lax.axis_index('tp')
     ep = lax.axis_index('ep')
     core = ep % 2
@@ -109,9 +110,11 @@
         rows = pl.ds(pl.multiple_of(r * block_rows, block_rows), block_rows)
         x_ref[rows, :] = rms_norm(h_ref[rows, :].astype(jnp.float32), gain_a_ref[...]).astype(jnp.bfloat16)
         return carry
-    lax.fori_loop(0, tokens // block_rows, attn_norm, 0)
 
     pl.semaphore_wait(barrier, 4)
+
+    def recv_wait(dst, sem):
+        pltpu.make_async_copy(dst, dst, sem).wait()
 
     def remote(src, dst, ssem, rsem, dev):
         return pltpu.make_async_remote_copy(src_ref=src, dst_ref=dst, send_sem=ssem, recv_sem=rsem, device_id=dev, device_id_type=MESH_ID)
@@ -120,13 +123,27 @@
         return gt_ref.at[pl.ds(pl.multiple_of((shard * 2 + tp) * n_local, n_local), n_local)]
 
     g_sends = [remote(gate_rows(peer), gates.at[ep], g_ssem.at[k], g_rsem.at[ep], {'ep': peer}) for k, peer in enumerate((mate, across, diagonal))]
-    x_sends = [remote(x_ref, x_all.at[ep], x_ssem.at[k], x_rsem.at[ep], {'ep': peer}) for k, peer in enumerate((mate, across))]
+    chunk_rows = tokens // CHUNKS
+
+    def chunk(src, c):
+        return x_all.at[src, pl.ds(c * chunk_rows, chunk_rows)]
+
+    def x_recv(src):
+        for c in range(CHUNKS):
+            recv_wait(chunk(src, c), x_rsem.at[src, c])
+
+    x_sends = [[remote(chunk(ep, c), chunk(ep, c), x_ssem.at[k, c], x_rsem.at[ep, c], {'ep': peer}) for k, peer in enumerate((across, mate))] for c in range(CHUNKS)]
+    x_fwd = [remote(chunk(across, c), chunk(across, c), x_ssem.at[2, c], x_rsem.at[across, c], {'ep': mate}) for c in range(CHUNKS)]
     a_send = remote(attn_ref, attn_rx, a_sem.at[0], a_sem.at[1], {'tp': 1 - tp})
     start(g_sends)
-    start(x_sends)
-
-    def recv_wait(dst, sem):
-        pltpu.make_async_copy(dst, dst, sem).wait()
+    blocks = chunk_rows // block_rows
+    for c in range(CHUNKS):
+        lax.fori_loop(c * blocks, (c + 1) * blocks, attn_norm, 0, unroll=True)
+        start(x_sends[c])
+
+    def forward(c):
+        recv_wait(chunk(across, c), x_rsem.at[across, c])
+        x_fwd[c].start()
 
     lane = lax.broadcasted_iota(jnp.int32, (tokens, tokens), 1)
     row = lax.broadcasted_iota(jnp.int32, (tokens, tokens), 0)
@@ -169,6 +186,11 @@
     cache_pos = jnp.where(cache_lane % n_kv == head_row // group, cache_lane // n_kv, ctx_rows)
 
     def attend(i, carry):
+        for c in range(CHUNKS // 2):
+            @pl.when(i == n_batches - CHUNKS // 2 + c)
+            def _(c=c):
+                forward(c)
+
         first = i * BATCH
         base = (i % 2) * (BATCH // 2)
         wait(cache_copies(i, 0))
@@ -216,6 +238,7 @@
         return carry
     n_batches = tokens // BATCH
     lax.fori_loop(0, n_batches, attend, 0)
+    down_start(0, 0)
 
     for k in range(n_heads):
         o_rows[:, k * HEAD:(k + 1) * HEAD] = o_buf[:, k, :].astype(jnp.bfloat16)
@@ -225,19 +248,18 @@
         got = jnp.dot(o_rows[...], x_rows[:, :, cols].reshape(qw, TILE), preferred_element_type=jnp.float32)
         attn_ref[:, cols] = got.astype(jnp.bfloat16)
 
-    recv_wait(x_all.at[across], x_rsem.at[across])
-    x_fwd = remote(x_all.at[across], x_all.at[across], x_ssem.at[2], x_rsem.at[across], {'ep': mate})
-    x_fwd.start()
+    for c in range(CHUNKS // 2, CHUNKS):
+        forward(c)
 
     gates[ep] = gt_ref[pl.ds(pl.multiple_of((ep * 2 + tp) * n_local, n_local), n_local), :]
     dispatch(ep, x_ref)
     for src in (mate, across, diagonal):
         recv_wait(gates.at[src], g_rsem.at[src])
-    recv_wait(x_all.at[mate], x_rsem.at[mate])
+    x_recv(mate)
     dispatch(mate, x_all.at[mate])
     a_send.start()
     dispatch(across, x_all.at[across])
-    recv_wait(x_all.at[diagonal], x_rsem.at[diagonal])
+    x_recv(diagonal)
     dispatch(diagonal, x_all.at[diagonal])
 
     def gate_up(lhs, slot, dst):
@@ -269,7 +291,7 @@
         return carry
     lax.fori_loop(0, n_local, expert, 0)
     shared_slot = n_local % 2
-    down_start(0, 0)
+    down_start(1, 1)
 
     recv_wait(attn_rx, a_sem.at[1])
 
@@ -280,10 +302,9 @@
         attn_sum[rows, :] = res
         y_norm[rows, :] = rms_norm(res, gain_f_ref[...]).astype(jnp.bfloat16)
         return carry
-    lax.fori_loop(0, tokens // block_rows, ffn_norm, 0)
+    lax.fori_loop(0, tokens // block_rows, ffn_norm, 0, unroll=4)
     wait(shared_copies(shared_slot))
     gate_up(y_norm, shared_slot, n_local)
-    down_start(1, 1)
 
     def split3(v):
         a = v.astype(jnp.bfloat16)
@@ -305,10 +326,6 @@
 
     def s3_copy(i):
         return remote(send3.at[i], recv3.at[i], s3_sem.at[i], r3_sem.at[i], {'tp': 1 - tp})
-
-    def out_copy(i):
-        cols = pl.ds(pl.multiple_of(i * TILE, TILE), TILE)
-        return pltpu.make_async_copy(out_buf.at[:, cols], out_ref.at[:, cols], out_sem.at[i])
 
     def down_tile(i, slot):
         base = slot * (n_local + 1)
@@ -358,19 +375,17 @@
             cols = pl.ds(pl.multiple_of(k * TILE, TILE), TILE)
             recv_wait(recv3.at[k], r3_sem.at[k])
             ffn = send3[k].astype(jnp.float32) + recv3[k].astype(jnp.float32)
-            out_buf[:, cols] = (attn_sum[:, cols] + ffn).astype(jnp.bfloat16)
-            out_copy(k).start()
+            out_ref[:, cols] = (attn_sum[:, cols] + ffn).astype(jnp.bfloat16)
         return carry
     lax.fori_loop(0, n_tiles + LAG3, step, 0)
 
-    for c in g_sends + x_sends + [x_fwd, a_send]:
+    for c in g_sends + sum(x_sends, x_fwd) + [a_send]:
         c.wait_send()
 
     def drain(i, carry):
         s1_copy(i).wait_send()
         s2_copy(i).wait_send()
         s3_copy(i).wait_send()
-        out_copy(i).wait()
         return carry
     lax.fori_loop(0, n_tiles, drain, 0)
 
@@ -392,9 +407,9 @@
     caches = [c.reshape(tokens // 2, 2 * ctx_len * n_kv, HEAD) for c in (k_cache, v_cache)]
     return pl.pallas_call(
         layer_kernel,
-        out_shape=jax.ShapeDtypeStruct((tokens, d_model), bf16),
+        out_shape=pltpu.VMEM((tokens, d_model), bf16),
         in_specs=[hbm] * 18,
-        out_specs=hbm,
+        out_specs=pl.BlockSpec(memory_space=pltpu.VMEM),
         scratch_shapes=[
             pltpu.VMEM((4, tokens, d_model), bf16),
             pltpu.VMEM((n_local, 4 * SLOT, d_model), bf16),
@@ -411,13 +426,13 @@
             pltpu.VMEM((4, n_local, tokens), f32),
             pltpu.VMEM((n_local * shards, tokens), f32),
             pltpu.SMEM((tokens,), jnp.int32), rows_bf16, pltpu.VMEM((1, d_model), f32), pltpu.VMEM((1, d_model), f32),
-            pltpu.VMEM(expert_ids.shape[::-1], jnp.int32), pltpu.VMEM(gate_vals.shape[::-1], f32), rows_bf16,
+            pltpu.VMEM(expert_ids.shape[::-1], jnp.int32), pltpu.VMEM(gate_vals.shape[::-1], f32),
             heads, heads, heads, heads,
             pltpu.VMEM((BATCH * n_heads, ctx_len * n_kv), f32),
             pltpu.VMEM((tokens, n_heads * HEAD), bf16),
             pair_tile, pair_tile, tile, tile, tile, tile, tile_f32, tile_f32,
-            dma((2, 2)), dma((2, 4)), dma((2, BATCH // 2, 2)), dma((4,)), dma((3,)), dma((4,)), dma((3,)), dma((4,)), dma((2,)),
-        ] + [dma((n_tiles,))] * 6 + [dma((6,)), dma((n_tiles,))],
+            dma((2, 2)), dma((2, 4)), dma((2, BATCH // 2, 2)), dma((4,)), dma((3, CHUNKS)), dma((4, CHUNKS)), dma((3,)), dma((4,)), dma((2,)),
+        ] + [dma((n_tiles,))] * 6 + [dma((6,))],
         compiler_params=pltpu.CompilerParams(collective_id=0, has_side_effects=True, vmem_limit_bytes=63 * 1024 * 1024),
         cost_estimate=pl.CostEstimate(flops=2 * tokens * (n_local + 1) * 3 * d_model * hidden_dim, bytes_accessed=(n_local + 1) * 6 * d_model * hidden_dim, transcendentals=0),
         name='layer',

time: 87.4 us -> 85.2 us (0.975)
  Pallas kernels: 85.4 us -> 84.3 us
  local copies, waits for them, and re-layouts: 1.88 us -> 0.8 us
    unnamed x1, local copies, waits for them, and re-layouts: 1.88 us -> 0.8 us
    pallas_call x1, Pallas kernels: 85.4 us -> 84.3 us  [fused_layer(): pl.pallas_call(layer_kernel, out_shape=pltpu.VMEM((tokens, d_model), bf16...]
where the time goes in v6:
time: 85.2 us; the launch traced here: 85.1 us
  Pallas kernels  84.3 us (99%)
    pallas_call x1, Pallas kernels, fused_layer(): pl.pallas_call(layer_kernel, out_shape=pltpu.VMEM((tokens, d_model), bf16...  84.3 us

profile of v6, /device:TPU:0, one launch (start us, length us, event | category | flops | bytes accessed | tf_op | source)
XLA Modules:
  0.0 85.1 jit_solution(9717598689683353717)
XLA Ops:
  0.0 84.3 %layer.1 = bf16[128,2048]{1,0:T(8,128)(2,1)S(1)} custom-call(s32[128]{0:T(128)} %len_in.1, bf16[128,2048]{1,0:T(8,128)(2,1)} %h_in.1, f32[1,2048]{1,0:T(1,128)} %bitcast.10, f32[1,2048]{1,0:T(1,128)} %bitcast.11, s32[6,128]{1,0:T(8,128)} %bitcast.12, f32[6,128]{1,0:T(8,128)} %bitcast.13, bf16[2048,1024]{1,0:T(8,128)(2,1)} %wq_ref.1, ...), custom_call_target="tpu_custom_call" | custom-call | flops 19931332608 | bytes 155713536 | tf_op jit(solution)/shard_map/layer/pallas_call | solution.py:408
  84.3 0.8 copy.20

commit v7 on v6

--- a/solution.py
+++ b/solution.py
@@ -248,15 +248,15 @@
         got = jnp.dot(o_rows[...], x_rows[:, :, cols].reshape(qw, TILE), preferred_element_type=jnp.float32)
         attn_ref[:, cols] = got.astype(jnp.bfloat16)
 
-    for c in range(CHUNKS // 2, CHUNKS):
-        forward(c)
-
     gates[ep] = gt_ref[pl.ds(pl.multiple_of((ep * 2 + tp) * n_local, n_local), n_local), :]
     dispatch(ep, x_ref)
+    for c in range(CHUNKS // 2, CHUNKS - 1):
+        forward(c)
     for src in (mate, across, diagonal):
         recv_wait(gates.at[src], g_rsem.at[src])
     x_recv(mate)
     dispatch(mate, x_all.at[mate])
+    forward(CHUNKS - 1)
     a_send.start()
     dispatch(across, x_all.at[across])
     x_recv(diagonal)

time: 85.2 us -> 85.9 us (level)
  no operation moved by 1% of the time
where the time goes in v7:
time: 85.9 us; the launch traced here: 85.8 us
  Pallas kernels  85 us (99%)
    pallas_call x1, Pallas kernels, fused_layer(): pl.pallas_call(layer_kernel, out_shape=pltpu.VMEM((tokens, d_model), bf16...  85 us

profile of v7, /device:TPU:0, one launch (start us, length us, event | category | flops | bytes accessed | tf_op | source)
XLA Modules:
  0.0 85.8 jit_solution(1666720055850131089)
XLA Ops:
  0.0 85.0 %layer.1 = bf16[128,2048]{1,0:T(8,128)(2,1)S(1)} custom-call(s32[128]{0:T(128)} %len_in.1, bf16[128,2048]{1,0:T(8,128)(2,1)} %h_in.1, f32[1,2048]{1,0:T(1,128)} %bitcast.10, f32[1,2048]{1,0:T(1,128)} %bitcast.11, s32[6,128]{1,0:T(8,128)} %bitcast.12, f32[6,128]{1,0:T(8,128)} %bitcast.13, bf16[2048,1024]{1,0:T(8,128)(2,1)} %wq_ref.1, ...), custom_call_target="tpu_custom_call" | custom-call | flops 19931332608 | bytes 155713536 | tf_op jit(solution)/shard_map/layer/pallas_call | solution.py:408
  85.0 0.8 copy.20

commit v8 on v6

--- a/solution.py
+++ b/solution.py
@@ -327,9 +327,10 @@
     def s3_copy(i):
         return remote(send3.at[i], recv3.at[i], s3_sem.at[i], r3_sem.at[i], {'tp': 1 - tp})
 
-    def down_tile(i, slot):
+    def down_tile(i, slot, refill):
         base = slot * (n_local + 1)
-        now, later = down_copies(i, slot), down_copies(i + 2, slot)
+        now = down_copies(i, slot)
+        later = down_copies(i + 2, slot) if refill else None
         for k in range(len(now)):
             wait(now[k])
             for j in range(k * GROUP, min((k + 1) * GROUP, n_local)):
@@ -340,8 +341,7 @@
             if k == len(now) - 1:
                 keep_own[i] = jnp.dot(act[n_local], down[base + n_local], preferred_element_type=jnp.float32)
 
-            @pl.when(i + 2 < n_tiles)
-            def _(k=k):
+            if refill:
                 start(later[k])
         for b in range(2):
             send1[i, b] = combine(b * 2 + 1 - core).astype(jnp.bfloat16)
@@ -349,10 +349,13 @@
         keep_other[i] = combine((1 - chip) * 2 + core)
         keep_own[i] = keep_own[i] + combine(ep)
 
-    def step(i, carry):
-        @pl.when(i < n_tiles)
-        def _():
-            down_tile(i, i % 2)
+    def step(i, carry, refill):
+        if refill:
+            down_tile(i, i % 2, True)
+        else:
+            @pl.when(i < n_tiles)
+            def _():
+                down_tile(i, i % 2, False)
 
         @pl.when((i >= LAG1) & (i < n_tiles + LAG1))
         def _():
@@ -377,7 +380,8 @@
             ffn = send3[k].astype(jnp.float32) + recv3[k].astype(jnp.float32)
             out_ref[:, cols] = (attn_sum[:, cols] + ffn).astype(jnp.bfloat16)
         return carry
-    lax.fori_loop(0, n_tiles + LAG3, step, 0)
+    lax.fori_loop(0, n_tiles - 2, functools.partial(step, refill=True), 0)
+    lax.fori_loop(n_tiles - 2, n_tiles + LAG3, functools.partial(step, refill=False), 0)
 
     for c in g_sends + sum(x_sends, x_fwd) + [a_send]:
         c.wait_send()

time: 85.2 us -> 85.2 us (level)
  no operation moved by 1% of the time
where the time goes in v8:
time: 85.2 us; the launch traced here: 85.1 us
  Pallas kernels  84.3 us (99%)
    pallas_call x1, Pallas kernels, fused_layer(): pl.pallas_call(layer_kernel, out_shape=pltpu.VMEM((tokens, d_model), bf16...  84.3 us

profile of v8, /device:TPU:0, one launch (start us, length us, event | category | flops | bytes accessed | tf_op | source)
XLA Modules:
  0.0 85.1 jit_solution(12759810414808434726)
XLA Ops:
  0.0 84.3 %layer.1 = bf16[128,2048]{1,0:T(8,128)(2,1)S(1)} custom-call(s32[128]{0:T(128)} %len_in.1, bf16[128,2048]{1,0:T(8,128)(2,1)} %h_in.1, f32[1,2048]{1,0:T(1,128)} %bitcast.10, f32[1,2048]{1,0:T(1,128)} %bitcast.11, s32[6,128]{1,0:T(8,128)} %bitcast.12, f32[6,128]{1,0:T(8,128)} %bitcast.13, bf16[2048,1024]{1,0:T(8,128)(2,1)} %wq_ref.1, ...), custom_call_target="tpu_custom_call" | custom-call | flops 19931332608 | bytes 155713536 | tf_op jit(solution)/shard_map/layer/pallas_call | solution.py:412
  84.3 0.8 copy.20
